TPU v7x, 512 devices: a whole 4x8x8 slice. The times are simulated.
512 devices in a mesh: dp: 128 (over y, z, core), feat: 4 (over x).
Axes of the slice: x: 4, y: 8, z: 8, core: 2. Of those that a mesh axis runs over, the one named last changes fastest.
Arguments:
- observations: bfloat16 [16384, 128, 128], P('dp', 'feat'), may hold values from -1.5 to 1.5
- labels: int32 [16384, 128], P('dp'), may hold values 0 or 1
- tile_live: int32 [16384], P('dp'), may hold values from 1 to 128
- tile_group: int32 [16384], P('dp'), may hold values from 0 to 2047, as said below
- position: float32 [2048, 2048], P('dp', 'feat'), may hold values from -2.4 to 2.4
- momentum: float32 [2048, 2048], P('dp', 'feat'), may hold values from -6 to 6
- gradient: float32 [2048, 2048], P('dp', 'feat'), may hold values from -18 to 18
- prior_mean: float32 [2048], P('feat'), may hold values from -1.8 to 1.8
- prior_prec: float32 [128], P('feat'), may hold values from 0.25 to 4
- inv_mass: float32 [128], P('feat'), may hold values from 0.5 to 2
Outputs:
- new_position: float32 [2048, 2048], P('dp', 'feat')
- new_momentum: float32 [2048, 2048], P('dp', 'feat')
- new_gradient: float32 [2048, 2048], P('dp', 'feat')
- energy: float32 [2048, 16], P('dp')
Inputs may be any that keep to these rules, and one draw needn't show every extreme that they name: `tile_group`: group g belongs to owner g // 16. Among the 128 tiles of one device at most 2 have groups of any one owner, and one owner has exactly 2 tiles from every device. `tile_live`: the live slots of a tile come first.
All inputs are finite; a program needn't handle non-finite values. No bound on the sum of `labels` on one device may be relied on, other than what follows from the above.
Results may differ from a plain program's by a relative error of at most 0.0041.
Values may be sent and summed in bfloat16 or wider, within the bound.
A program may use at most 64 MiB of HBM per device.

v0:
```python
import jax
import jax.numpy as jnp
from jax import lax
from jax.sharding import PartitionSpec as P

step_size = 0.1


def cut_along(shard, dim, size):
    dims = shard.shape
    pieces = shard.reshape(*dims[:dim], size, dims[dim] // size, *dims[dim + 1 :])
    return jnp.moveaxis(pieces, dim, 0)


def sent_and_summed(shard, axis, dim):
    pieces = cut_along(shard, dim, lax.axis_size(axis))
    arrived = lax.all_to_all(pieces, axis, split_axis=0, concat_axis=0, tiled=True)
    return arrived.astype(jnp.float32).sum(axis=0)


def laid_out(pieces, dim):
    dims = list(pieces.shape[1:])
    dims[dim] *= pieces.shape[0]
    return jnp.moveaxis(pieces, 0, dim).reshape(dims)


def from_everyone(shard, axis):
    copies = jnp.broadcast_to(shard, (lax.axis_size(axis), *shard.shape))
    return lax.all_to_all(copies, axis, split_axis=0, concat_axis=0, tiled=True)


def gathered_copies(shard, axis, dim):
    return laid_out(from_everyone(shard, axis), dim)


def sent_together(arrays, axis, split_dim, concat_dim, along):
    ends, at = ([], 0)
    for a in arrays[:-1]:
        at += a.shape[along]
        ends.append(at)
    both = jnp.concatenate(arrays, axis=along)
    return tuple(
        jnp.split(
            lax.all_to_all(both, axis, split_axis=split_dim, concat_axis=concat_dim, tiled=True),
            ends,
            axis=along,
        )
    )


def likelihood(logits, labels, tile_live):
    row_count = logits.shape[2]
    live_rows = (jnp.arange(row_count, dtype=jnp.int32)[None, :] < tile_live[:, None])[:, None, :]
    targets = labels.astype(jnp.float32)[:, None, :]
    residual = jnp.where(live_rows, jax.nn.sigmoid(logits) - targets, 0.0).astype(jnp.bfloat16)
    neg_loglik = jnp.sum(
        jnp.where(live_rows, jax.nn.softplus(logits) - targets * logits, 0.0), axis=2
    )
    return (residual, neg_loglik)


def body(
    observations,
    labels,
    tile_live,
    tile_group,
    position,
    momentum,
    gradient,
    prior_mean,
    prior_prec,
    inv_mass,
):
    owners = lax.axis_size("dp")
    owner_index = lax.axis_index("dp")
    tile_count, quarter, row_count = observations.shape
    own_groups = position.shape[0]
    block_width = position.shape[1]
    chains = block_width // quarter
    slot_count = max(2, 2 * tile_count // owners)
    prior_full = jnp.repeat(prior_prec, chains)
    mass_full = jnp.repeat(inv_mass, chains)
    half_momentum = momentum - 0.5 * step_size * gradient
    moved_position = position + step_size * mass_full * half_momentum
    rounded = moved_position.astype(jnp.bfloat16)
    target = tile_group // own_groups
    tile_order = jnp.arange(tile_count, dtype=jnp.int32)
    earlier = (target[:, None] == target[None, :]) & (tile_order[None, :] < tile_order[:, None])
    slot_rank = jnp.sum(earlier.astype(jnp.int32), axis=1)
    slot_place = target * slot_count + slot_rank
    slot_tile = jnp.full((owners * slot_count,), -1, jnp.int32).at[slot_place].set(tile_order)
    filled = slot_tile >= 0
    safe_tile = jnp.maximum(slot_tile, 0)
    requests = jnp.where(filled, tile_group[safe_tile], -1).reshape(owners, slot_count)
    group_order = jnp.arange(own_groups, dtype=jnp.int32)
    asked_groups = lax.all_to_all(requests, "dp", split_axis=0, concat_axis=0, tiled=True)
    local_group = asked_groups - owner_index * own_groups
    selector = (local_group[:, :, None] == group_order[None, None, :]).astype(jnp.bfloat16)
    picked = jnp.einsum(
        "nkg,gw->nkw", selector, rounded, preferred_element_type=jnp.float32
    ).astype(jnp.bfloat16)
    fetched = lax.all_to_all(picked, "dp", split_axis=0, concat_axis=0, tiled=True)
    tile_blocks = fetched.reshape(owners * slot_count, block_width)[slot_place]
    tile_coeffs = tile_blocks.reshape(tile_count, quarter, chains)
    partial_logits = jnp.einsum(
        "tfc,tfr->tcr", tile_coeffs, observations, preferred_element_type=jnp.float32
    )
    logit_share = sent_and_summed(partial_logits.astype(jnp.bfloat16), "feat", 0)
    share_count = logit_share.shape[0]
    share_start = lax.axis_index("feat") * share_count
    share_labels = lax.dynamic_slice_in_dim(labels, share_start, share_count, 0)
    share_live = lax.dynamic_slice_in_dim(tile_live, share_start, share_count, 0)
    residual_share, loglik_share = likelihood(logit_share, share_labels, share_live)
    residual = gathered_copies(residual_share, "feat", 0)
    neg_loglik = lax.dynamic_update_slice_in_dim(
        jnp.zeros((tile_count, chains), jnp.float32), loglik_share, share_start, 0
    )
    partial_grad = jnp.einsum(
        "tfr,tcr->tfc", observations, residual, preferred_element_type=jnp.float32
    ).reshape(tile_count, block_width)
    send_grad = jnp.where(filled[:, None], partial_grad[safe_tile], 0.0).reshape(
        owners, slot_count, block_width
    )
    send_loglik = jnp.where(filled[:, None], neg_loglik[safe_tile], 0.0).reshape(
        owners, slot_count, chains
    )
    got_grad, got_loglik = tuple(
        (
            part.astype(jnp.float32)
            for part in sent_together(
                (send_grad.astype(jnp.bfloat16), send_loglik.astype(jnp.bfloat16)), "dp", 0, 0, 2
            )
        )
    )
    local_slot = asked_groups.reshape(-1) - owner_index * own_groups
    collector = (group_order[:, None] == local_slot[None, :]).astype(jnp.float32)
    likelihood_grad = jnp.dot(
        collector,
        got_grad.reshape(-1, block_width),
        precision=lax.Precision.HIGHEST,
        preferred_element_type=jnp.float32,
    )
    group_loglik = jnp.dot(
        collector,
        got_loglik.reshape(-1, chains),
        precision=lax.Precision.HIGHEST,
        preferred_element_type=jnp.float32,
    )
    offset = moved_position - prior_mean
    new_gradient = likelihood_grad + prior_full * offset
    new_momentum = half_momentum - 0.5 * step_size * new_gradient
    quadratic = 0.5 * (prior_full * offset * offset + mass_full * new_momentum * new_momentum)
    quadratic = jnp.sum(quadratic.reshape(own_groups, quarter, chains), axis=1)
    summed = quadratic + group_loglik
    energy = lax.psum(summed, "feat")
    return (moved_position, new_momentum, new_gradient, energy)


def solution(mesh):
    placed = (
        P("dp", "feat", None),
        P("dp", None),
        P("dp"),
        P("dp"),
        P("dp", "feat"),
        P("dp", "feat"),
        P("dp", "feat"),
        P("feat"),
        P("feat"),
        P("feat"),
    )
    return jax.shard_map(
        body,
        mesh=mesh,
        in_specs=placed,
        out_specs=(P("dp", "feat"), P("dp", "feat"), P("dp", "feat"), P("dp", None)),
        check_vma=False,
    )
```

profile of v0, /device:TPU:1, one launch (start us, length us, event | category | flops | bytes accessed | tf_op | source)
XLA Modules:
  0.0 124.1 jit_solution(3307524245578154745)
XLA Ops:
  0.6 0.8 and_select_fusion
  1.6 0.5 copy-done.1
  2.1 1.0 scatter_custom_fusion
  3.1 1.9 %gather_fusion = s32[256]{0:T(256)S(1)} fusion(s32[128]{0:T(128)S(1)} %copy-done.1, s32[1024]{0:T(1024)S(1)} %pad_clamp_fusion.1), kind=kCustom, calls=%fused_computation | custom fusion | bytes 3072 | tf_op jit(solution)/shard_map/gather | solution.py:94
  5.0 0.8 all_to_all.18
  5.7 18.5 %all-to-all-start = ((s32[128,1,2]{2,1,0:T(1,128)}), s32[128,1,2]{2,1,0:T(1,128)S(1)}, u32[]{:S(2)}, u32[]{:S(2)}) async-start(s32[128,1,2]{2,1,0:T(1,128)} %bitcast), calls=%async_computation | async-start | bytes 131072 | tf_op jit(solution)/shard_map/all_to_all | solution.py:96
  24.5 0.6 copy-done.3
  25.1 10.7 %all-to-all-done = s32[128,1,2]{2,1,0:T(1,128)S(1)} async-done(((s32[128,1,2]{2,1,0:T(1,128)}), s32[128,1,2]{2,1,0:T(1,128)S(1)}, u32[]{:S(2)}, u32[]{:S(2)}) %all-to-all-start) | async-done | bytes 1056 | tf_op jit(solution)/shard_map/all_to_all | solution.py:96
  35.8 0.5 broadcast.89
  36.3 0.8 fusion.13
  37.5 1.0 copy.30
  38.5 5.7 %all-to-all-start.1 = ((bf16[128,2,512]{2,1,0:T(2,128)(2,1)}), bf16[128,2,512]{2,1,0:T(2,128)(2,1)S(1)}, u32[]{:S(2)}, u32[]{:S(2)}) async-start(bf16[128,2,512]{2,1,0:T(2,128)(2,1)} %copy.30), calls=%async_computation.1 | async-start | bytes 524288 | tf_op jit(solution)/shard_map/all_to_all | solution.py:102
  44.2 14.3 %all-to-all-done.1 = bf16[128,2,512]{2,1,0:T(2,128)(2,1)S(1)} async-done(((bf16[128,2,512]{2,1,0:T(2,128)(2,1)}), bf16[128,2,512]{2,1,0:T(2,128)(2,1)S(1)}, u32[]{:S(2)}, u32[]{:S(2)}) %all-to-all-start.1) | async-done | bytes 262176 | tf_op jit(solution)/shard_map/all_to_all | solution.py:102
  58.6 0.8 gather_fusion.1
  60.1 1.2 convolution_convert_fusion
  61.3 4.0 %all-to-all-start.2 = ((bf16[4,32,16,128]{3,2,1,0:T(8,128)(2,1)}), bf16[4,32,16,128]{3,2,1,0:T(8,128)(2,1)S(1)}, u32[]{:S(2)}, u32[]{:S(2)}) async-start(bf16[4,32,16,128]{3,2,1,0:T(8,128)(2,1)} %bitcast.4), calls=%async_computation.2 | async-start | bytes 1048576 | tf_op jit(solution)/shard_map/all_to_all | solution.py:17
  65.3 0.7 copy-done.9
  66.1 0.7 dynamic-slice_convert_fusion
  66.9 5.7 %all-to-all-done.2 = bf16[4,32,16,128]{3,2,1,0:T(8,128)(2,1)S(1)} async-done(((bf16[4,32,16,128]{3,2,1,0:T(8,128)(2,1)}), bf16[4,32,16,128]{3,2,1,0:T(8,128)(2,1)S(1)}, u32[]{:S(2)}, u32[]{:S(2)}) %all-to-all-start.2) | async-done | bytes 524320 | tf_op jit(solution)/shard_map/all_to_all | solution.py:17
  73.0 0.9 broadcast_in_dim.92
  73.9 3.5 %all-to-all-start.3 = ((bf16[4,32,16,128]{3,2,1,0:T(8,128)(2,1)}), bf16[4,32,16,128]{3,2,1,0:T(8,128)(2,1)S(1)}, u32[]{:S(2)}, u32[]{:S(2)}) async-start(bf16[4,32,16,128]{3,2,1,0:T(8,128)(2,1)} %broadcast_in_dim.92), calls=%async_computation.3 | async-start | bytes 1048576 | tf_op jit(solution)/shard_map/all_to_all | solution.py:29
  77.5 0.9 gather_fusion.3
  78.6 5.6 %all-to-all-done.3 = bf16[4,32,16,128]{3,2,1,0:T(8,128)(2,1)S(1)} async-done(((bf16[4,32,16,128]{3,2,1,0:T(8,128)(2,1)}), bf16[4,32,16,128]{3,2,1,0:T(8,128)(2,1)S(1)}, u32[]{:S(2)}, u32[]{:S(2)}) %all-to-all-start.3) | async-done | bytes 524320 | tf_op jit(solution)/shard_map/all_to_all | solution.py:29
  84.2 0.7 convolution_bitcast_fusion
  84.9 0.5 copy.33
  85.5 1.2 gather_fusion.2
  87.1 1.0 pad_maximum_fusion
  88.2 10.8 %all-to-all-start.4 = ((bf16[128,2,528]{2,1,0:T(2,128)(2,1)}), bf16[128,2,528]{2,1,0:T(2,128)(2,1)S(1)}, u32[]{:S(2)}, u32[]{:S(2)}) async-start(bf16[128,2,528]{2,1,0:T(2,128)(2,1)} %pad_maximum_fusion), calls=%async_computation.4 | async-start | bytes 655360 | tf_op jit(solution)/shard_map/all_to_all | solution.py:44
  99.3 15.2 %all-to-all-done.4 = bf16[128,2,528]{2,1,0:T(2,128)(2,1)S(1)} async-done(((bf16[128,2,528]{2,1,0:T(2,128)(2,1)}), bf16[128,2,528]{2,1,0:T(2,128)(2,1)S(1)}, u32[]{:S(2)}, u32[]{:S(2)}) %all-to-all-start.4) | async-done | bytes 270368 | tf_op jit(solution)/shard_map/all_to_all | solution.py:44
  114.9 0.6 copy-done.6
  115.4 0.8 fusion.5
  116.6 7.5 %psum.7 = f32[16,16]{1,0:T(8,128)} all-reduce(f32[16,16]{1,0:T(8,128)S(1)} %convolution_add_fusion.1), channel_id=1, replica_groups=mesh['dp'=128,'feat'=4] {'feat'}, use_global_device_ids=true, to_apply=%region_5.6 | all-reduce | flops 256 | bytes 2048 | tf_op jit(solution)/shard_map/psum | solution.py:155
  (52 shorter events, 3.8 us)
Async XLA Ops:
  0.6 59.5 %copy-start = (bf16[128,32,128]{2,1,0:T(8,128)(2,1)S(1)}, bf16[128,32,128]{2,1,0:T(8,128)(2,1)}, u32[]{:S(2)}) copy-start(bf16[128,32,128]{2,1,0:T(8,128)(2,1)} %param.10) | copy-start | bytes 3145732
  1.4 0.7 copy-start.1
  5.7 18.6 %copy-start.7 = (f32[32]{0:T(128)S(1)}, f32[32]{0:T(128)}, u32[]{:S(2)}) copy-start(f32[32]{0:T(128)} %param.19) | copy-start | bytes 388
  5.7 18.7 %copy-start.4 = (f32[16,512]{1,0:T(8,128)S(1)}, f32[16,512]{1,0:T(8,128)}, u32[]{:S(2)}) copy-start(f32[16,512]{1,0:T(8,128)} %param.16) | copy-start | bytes 98308
  5.7 18.7 %copy-start.5 = (f32[16,512]{1,0:T(8,128)S(1)}, f32[16,512]{1,0:T(8,128)}, u32[]{:S(2)}) copy-start(f32[16,512]{1,0:T(8,128)} %param.14) | copy-start | bytes 98308
  5.7 30.1 %all-to-all-start = ((s32[128,1,2]{2,1,0:T(1,128)}), s32[128,1,2]{2,1,0:T(1,128)S(1)}, u32[]{:S(2)}, u32[]{:S(2)}) async-start(s32[128,1,2]{2,1,0:T(1,128)} %bitcast), calls=%async_computation | async-start | bytes 131072 | tf_op jit(solution)/shard_map/all_to_all | solution.py:96
  24.3 0.8 copy-start.3
  25.1 89.8 %copy-start.2 = (f32[16,512]{1,0:T(8,128)}, f32[16,512]{1,0:T(8,128)S(1)}, u32[]{:S(2)}) copy-start(f32[16,512]{1,0:T(8,128)S(1)} %multiply_add_fusion) | copy-start | bytes 98308
  38.5 20.0 %all-to-all-start.1 = ((bf16[128,2,512]{2,1,0:T(2,128)(2,1)}), bf16[128,2,512]{2,1,0:T(2,128)(2,1)S(1)}, u32[]{:S(2)}, u32[]{:S(2)}) async-start(bf16[128,2,512]{2,1,0:T(2,128)(2,1)} %copy.30), calls=%async_computation.1 | async-start | bytes 524288 | tf_op jit(solution)/shard_map/all_to_all | solution.py:102
  61.3 11.3 %all-to-all-start.2 = ((bf16[4,32,16,128]{3,2,1,0:T(8,128)(2,1)}), bf16[4,32,16,128]{3,2,1,0:T(8,128)(2,1)S(1)}, u32[]{:S(2)}, u32[]{:S(2)}) async-start(bf16[4,32,16,128]{3,2,1,0:T(8,128)(2,1)} %bitcast.4), calls=%async_computation.2 | async-start | bytes 1048576 | tf_op jit(solution)/shard_map/all_to_all | solution.py:17
  65.3 0.7 copy-start.9
  73.9 10.4 %all-to-all-start.3 = ((bf16[4,32,16,128]{3,2,1,0:T(8,128)(2,1)}), bf16[4,32,16,128]{3,2,1,0:T(8,128)(2,1)S(1)}, u32[]{:S(2)}, u32[]{:S(2)}) async-start(bf16[4,32,16,128]{3,2,1,0:T(8,128)(2,1)} %broadcast_in_dim.92), calls=%async_computation.3 | async-start | bytes 1048576 | tf_op jit(solution)/shard_map/all_to_all | solution.py:29
  88.2 10.8 %copy-start.8 = (f32[32]{0:T(128)S(1)}, f32[32]{0:T(128)}, u32[]{:S(2)}) copy-start(f32[32]{0:T(128)} %param.18) | copy-start | bytes 388
  88.2 26.4 %all-to-all-start.4 = ((bf16[128,2,528]{2,1,0:T(2,128)(2,1)}), bf16[128,2,528]{2,1,0:T(2,128)(2,1)S(1)}, u32[]{:S(2)}, u32[]{:S(2)}) async-start(bf16[128,2,528]{2,1,0:T(2,128)(2,1)} %pad_maximum_fusion), calls=%async_computation.4 | async-start | bytes 655360 | tf_op jit(solution)/shard_map/all_to_all | solution.py:44
  114.8 0.7 copy-start.6
where the time goes:
time: 127 us; the launch traced here: 124 us
  waiting for transfers between devices  51.7 us (41%)
  starting transfers between devices  42.5 us (33%)
  local copies, waits for them, and re-layouts  13.7 us (11%)
  blocking collectives  7.54 us (6%)
  other arithmetic  4.6 us (4%)
  matrix products  3.07 us (2%)
    all_to_all x1, starting transfers between devices, body(): lax.all_to_all(requests, 'dp', split_axis=0, concat_axis=0, tiled=True)  18.5 us
    all_to_all x1, waiting for transfers between devices, sent_together(): lax.all_to_all(both, axis, split_axis=split_dim, concat_axis=concat_dim,...  15.2 us
    all_to_all x1, waiting for transfers between devices, body(): lax.all_to_all(picked, 'dp', split_axis=0, concat_axis=0, tiled=True)  14.3 us
    all_to_all x1, starting transfers between devices, sent_together(): lax.all_to_all(both, axis, split_axis=split_dim, concat_axis=concat_dim,...  10.8 us
    all_to_all x1, waiting for transfers between devices, body(): lax.all_to_all(requests, 'dp', split_axis=0, concat_axis=0, tiled=True)  10.7 us
    psum x1, blocking collectives, body(): energy = lax.psum(summed, 'feat')  7.54 us
    all_to_all x1, waiting for transfers between devices, sent_and_summed(): lax.all_to_all(pieces, axis, split_axis=0, concat_axis=0, tiled=True)  5.74 us
    all_to_all x1, starting transfers between devices, body(): lax.all_to_all(picked, 'dp', split_axis=0, concat_axis=0, tiled=True)  5.69 us
  transfers between devices with their start and end apart: 5, of which 5 were waited for; matrix products, arithmetic and copies ran while one was open for 2% of the time, Pallas kernels for 0%

commit v1 on v0

v1 whole, which is shorter than its diff:
```python
import functools

import jax
import jax.numpy as jnp
from jax import lax
from jax.experimental import pallas as pl
from jax.experimental.pallas import tpu as pltpu
from jax.sharding import PartitionSpec as P

MESH = pl.DeviceIdType.MESH
step_size = 0.1

NY = 8
NC = 2
CHAINS = 16
GRP = 16
LANES = 128
BF = jnp.bfloat16
F32 = jnp.float32


def far_first(n):
    return sorted(range(1, n), key=lambda i: -min(i, n - i))


def dot(a, b, contract=((1,), (0,))):
    return lax.dot_general(a, b, (contract, ((), ())), preferred_element_type=F32)


def one_hot(flags):
    return jnp.where(flags, 1.0, 0.0).astype(BF)


def kernel(
    obs,
    lab,
    live,
    tg,
    pos,
    mom,
    grd,
    pm,
    pp,
    im,
    new_pos,
    new_mom,
    new_grd,
    energy,
    obsx,
    perm,
    labf,
    mask,
    half_s,
    ltile,
    gat,
    rqs,
    rq,
    tmat,
    tmat_t,
    smat,
    smat_t,
    sels,
    selr,
    xs,
    xr,
    gs,
    gr,
    wf,
    gf,
    ms,
    mr,
    ys,
    yr,
    er,
    obs_ss,
    obs_rs,
    own_s,
    gat_ss,
    gat_rs,
    rq_ss,
    rq_rs,
    sel_ss,
    sel_rs,
    x_ss,
    x_rs,
    gx_ss,
    gx_rs,
    m_ss,
    m_rs,
    y_ss,
    y_rs,
    e_ss,
    e_rs,
):
    d = lax.axis_index("dp")
    k = lax.axis_index("feat")
    y, z, c = d // (NY * NC), (d // NC) % NY, d % NC
    tiles = lab.shape[0]
    nf = 4
    share = tiles // nf
    width = pos.shape[1]
    quarter = width // CHAINS
    half_w = width // 2

    def at(yy, zz, cc):
        return ((yy * NY + zz) * NC + cc, k)

    def xpeer(i):
        return (d, (k + i) % nf)

    g_me = (y, z)
    s_me = (z * NC + c, y * NC + c)

    def g_peer(a, i):
        return at((y + i) % NY, z, c) if a == 0 else at(y, (z + i) % NY, c)

    def s_peer(a, i):
        q = (s_me[a] + i) % (NY * NC)
        return at(y, q // NC, q % NC) if a == 0 else at(q // NC, z, q % NC)

    x_order = (2, 1, 3)
    g_order = far_first(NY)
    s_order = far_first(NY * NC)

    barrier = pltpu.get_barrier_semaphore()
    count = 0
    for i in x_order:
        pl.semaphore_signal(barrier, inc=1, device_id=xpeer(i), device_id_type=MESH)
        count += 1
    for zz in range(NY):
        for cc in range(NC):
            if (zz, cc) != (0, 0):
                who = at(y, (z + zz) % NY, (c + cc) % NC)
                pl.semaphore_signal(barrier, inc=1, device_id=who, device_id_type=MESH)
                count += 1
            if zz != 0:
                who = at((y + zz) % NY, z, (c + cc) % NC)
                pl.semaphore_signal(barrier, inc=1, device_id=who, device_id_type=MESH)
                count += 1

    src = lax.broadcasted_iota(jnp.int32, (LANES, width), 0)
    dst = lax.broadcasted_iota(jnp.int32, (LANES, width), 1)
    want = (dst % quarter) * CHAINS + dst // quarter
    for b in range(width // LANES):
        perm[b * LANES : (b + 1) * LANES, :] = one_hot(src + b * LANES == want)

    half = mom[...] - 0.5 * step_size * grd[...]
    moved = pos[...] + step_size * im[...] * half
    half_s[...] = half
    new_pos[...] = moved
    block = dot(moved.astype(BF), perm[...]).astype(BF)
    for a in range(2):
        gat[a, pl.ds(g_me[a], 1)] = block[None, :, a * half_w : (a + 1) * half_w]

    tile_row = jnp.broadcast_to(tg[...], (tiles, tiles))
    tile_col = jnp.transpose(tile_row.astype(F32)).astype(jnp.int32)
    own_row, own_col = tile_row // GRP, tile_col // GRP
    t_row = lax.broadcasted_iota(jnp.int32, (tiles, tiles), 1)
    t_col = lax.broadcasted_iota(jnp.int32, (tiles, tiles), 0)
    same = own_row == own_col
    rank_row = jnp.sum(jnp.where(same & (t_col < t_row), 1.0, 0.0), axis=0, keepdims=True)
    rank_row = jnp.broadcast_to(rank_row, (tiles, tiles))
    rank_col = jnp.transpose(rank_row).astype(jnp.int32)
    rank_row = rank_row.astype(jnp.int32)
    slots = NY * NC * NY * 2

    def slot_of(a, own, rank):
        oy, oz, oc = own // (NY * NC), (own // NC) % NY, own % NC
        first, second = (oy, oz) if a == 0 else (oz, oy)
        return (second * NC + oc) * (NY * 2) + first * 2 + rank, first

    for a in range(2):
        s_r, _ = slot_of(a, own_row, rank_row)
        s_c, first = slot_of(a, own_col, rank_col)
        asked = (first * GRP + tile_col % GRP + 1).astype(F32).astype(BF)
        for b in range(slots // LANES):
            tmat[a, :, b * LANES : (b + 1) * LANES] = one_hot(s_c == t_row + b * LANES)
            tmat_t[a, b * LANES : (b + 1) * LANES, :] = one_hot(s_r == t_col + b * LANES)
        rqs[a] = dot(tmat_t[a], asked).astype(BF).reshape(NY * NC, NY * 2, LANES)

    pl.semaphore_wait(barrier, count)

    copies = []

    def send(src_ref, dst_ref, ss, rs, who):
        copy = pltpu.make_async_remote_copy(
            src_ref=src_ref, dst_ref=dst_ref, send_sem=ss, recv_sem=rs, device_id=who, device_id_type=MESH
        )
        copy.start()
        copies.append(copy)
        return copy

    gat_c = [[], []]
    rq_c = [[], []]
    for a in range(2):
        for i in g_order:
            ref = gat.at[a, g_me[a]]
            gat_c[a].append(send(ref, ref, gat_ss.at[a, i], gat_rs.at[a, i], g_peer(a, i)))
    for a in range(2):
        for i in s_order:
            q = (s_me[a] + i) % (NY * NC)
            rq_c[a].append(send(rqs.at[a, q], rq.at[a, s_me[a]], rq_ss.at[a, i], rq_rs.at[a, i], s_peer(a, i)))
    obs_c = []
    for i in x_order:
        to = (k + i) % nf
        obs_c.append(
            send(
                obs.at[pl.ds(to * share, share)],
                obsx.at[:, pl.ds(pl.multiple_of(k * quarter, quarter), quarter), :],
                obs_ss.at[i],
                obs_rs.at[i],
                xpeer(i),
            )
        )
    own_copy = pltpu.make_async_copy(
        obs.at[pl.ds(k * share, share)],
        obsx.at[:, pl.ds(pl.multiple_of(k * quarter, quarter), quarter), :],
        own_s,
    )
    own_copy.start()

    rows = pl.ds(pl.multiple_of(k * share, share), share)
    labf[...] = lab[rows, :].astype(F32)
    live_col = jnp.transpose(jnp.broadcast_to(live[...], (tiles, tiles)).astype(F32))
    mask[...] = jnp.where(t_row.astype(F32) < live_col, 1.0, 0.0)
    ltile[...] = jnp.zeros_like(ltile)

    for a in range(2):
        rq[a, pl.ds(s_me[a], 1)] = rqs[a, pl.ds(s_me[a], 1)]
        for copy in rq_c[a]:
            copy.wait_recv()
        ask = rq[a].reshape(slots, LANES).astype(F32)
        lane1 = (lax.broadcasted_iota(jnp.int32, (slots, LANES), 1) + 1).astype(F32)
        chosen = jnp.where(ask == lane1, 1.0, 0.0)
        smat[a] = chosen.astype(BF)
        for b in range(slots // LANES):
            smat_t[a, :, b * LANES : (b + 1) * LANES] = jnp.transpose(
                chosen[b * LANES : (b + 1) * LANES, :]
            ).astype(BF)

    sel_c = [[], []]
    for a in range(2):
        for copy in gat_c[a]:
            copy.wait_recv()
        table = gat[a].reshape(NY * GRP, half_w)
        sels[a] = dot(smat[a], table).astype(BF).reshape(NY * NC, NY * 2, half_w)
        for i in s_order:
            q = (s_me[a] + i) % (NY * NC)
            sel_c[a].append(
                send(sels.at[a, q], selr.at[a, s_me[a]], sel_ss.at[a, i], sel_rs.at[a, i], s_peer(a, i))
            )
        selr[a, pl.ds(s_me[a], 1)] = sels[a, pl.ds(s_me[a], 1)]

    x_c = [[], []]
    for a in range(2):
        for copy in sel_c[a]:
            copy.wait_recv()
        rows_a = dot(tmat[a], selr[a].reshape(slots, half_w)).astype(BF)
        xs[a] = rows_a.reshape(nf, share, half_w)
        for i in x_order:
            to = (k + i) % nf
            x_c[a].append(send(xs.at[a, to], xr.at[a, k], x_ss.at[a, i], x_rs.at[a, i], xpeer(i)))
        xr[a, pl.ds(k, 1)] = xs[a, pl.ds(k, 1)]

    lane = lax.broadcasted_iota(jnp.int32, (share, LANES), 1) // quarter
    per = LANES // quarter
    for a in range(2):
        for copy in x_c[a]:
            copy.wait_recv()
        for b in range(half_w // LANES):
            came = [xr[a, kk, :, b * LANES : (b + 1) * LANES].astype(F32) for kk in range(nf)]
            for ci in range(per):
                out = jnp.zeros((share, LANES), F32)
                for kk in range(nf):
                    shift = ((kk - ci) * quarter) % LANES
                    moved_k = came[kk] if shift == 0 else pltpu.roll(came[kk], shift, 1)
                    out = jnp.where(lane == kk, moved_k, out)
                chain = a * (CHAINS // 2) + b * per + ci
                wf[chain * share : (chain + 1) * share, :] = out

    own_copy.wait()
    for copy in obs_c:
        copy.wait_recv()

    lane16 = lax.broadcasted_iota(jnp.int32, (CHAINS, LANES), 1)
    loglik = jnp.zeros((CHAINS, LANES), F32)
    base = k * share
    for t in range(share):
        coeff = wf[pl.ds(t, CHAINS, stride=share), :].astype(BF)
        tile = obsx[t]
        logits = dot(coeff, tile)
        target = jnp.broadcast_to(labf[t : t + 1, :], (CHAINS, LANES))
        alive = jnp.broadcast_to(mask[pl.ds(base + t, 1), :], (CHAINS, LANES)) > 0.5
        e = jnp.exp(-jnp.abs(logits))
        r = 1.0 / (1.0 + e)
        sig = jnp.where(logits >= 0.0, r, e * r)
        residual = jnp.where(alive, sig - target, 0.0).astype(BF)
        soft = jnp.maximum(logits, 0.0) + jnp.log1p(e)
        term = jnp.where(alive, soft - target * logits, 0.0)
        loglik = jnp.where(lane16 == t, jnp.sum(term, axis=1, keepdims=True), loglik)
        gf[pl.ds(t, CHAINS, stride=share), :] = dot(residual, tile, ((1,), (1,)))

    gx_c = [[], []]
    for a in range(2):
        for b in range(half_w // LANES):
            chain = a * (CHAINS // 2) + b * per
            made = [gf[(chain + ci) * share : (chain + ci + 1) * share, :] for ci in range(per)]
            for kk in range(nf):
                out = jnp.zeros((share, LANES), F32)
                for ci in range(per):
                    shift = ((ci - kk) * quarter) % LANES
                    moved_c = made[ci] if shift == 0 else pltpu.roll(made[ci], shift, 1)
                    out = jnp.where(lane == ci, moved_c, out)
                gs[a, kk, :, b * LANES : (b + 1) * LANES] = out.astype(BF)
        for i in x_order:
            to = (k + i) % nf
            gx_c[a].append(send(gs.at[a, to], gr.at[a, k], gx_ss.at[a, i], gx_rs.at[a, i], xpeer(i)))
        gr[a, pl.ds(k, 1)] = gs[a, pl.ds(k, 1)]

    high = loglik.astype(BF).astype(F32)
    both = jnp.concatenate([high, loglik - high, jnp.zeros((LANES - 2 * CHAINS, LANES), F32)], axis=0)
    ltile[rows, :] = jnp.transpose(both)[:share, :].astype(BF)

    m_c = [[], []]
    for a in range(2):
        for copy in gx_c[a]:
            copy.wait_recv()
        sent = dot(tmat_t[a], gr[a].reshape(tiles, half_w)).astype(BF)
        ms[a, :, :, :half_w] = sent.reshape(NY * NC, NY * 2, half_w)
        w = half_w
        if a == 0:
            ext = dot(tmat_t[a], ltile[...]).astype(BF)
            ms[a, :, :, half_w:] = ext.reshape(NY * NC, NY * 2, LANES)
            w = half_w + LANES
        for i in s_order:
            q = (s_me[a] + i) % (NY * NC)
            m_c[a].append(
                send(
                    ms.at[a, q, :, pl.ds(0, w)],
                    mr.at[a, s_me[a], :, pl.ds(0, w)],
                    m_ss.at[a, i],
                    m_rs.at[a, i],
                    s_peer(a, i),
                )
            )
        mr[a, pl.ds(s_me[a], 1), :, :w] = ms[a, pl.ds(s_me[a], 1), :, :w]

    y_c = [[], []]
    for a in range(2):
        w = half_w + LANES if a == 0 else half_w
        for copy in m_c[a]:
            copy.wait_recv()
        summed = dot(smat_t[a], mr[a, :, :, :w].reshape(slots, w)).astype(BF)
        ys[a, :, :, :w] = summed.reshape(NY, GRP, w)
        for i in g_order:
            to = (g_me[a] + i) % NY
            y_c[a].append(
                send(
                    ys.at[a, to, :, pl.ds(0, w)],
                    yr.at[a, g_me[a], :, pl.ds(0, w)],
                    y_ss.at[a, i],
                    y_rs.at[a, i],
                    g_peer(a, i),
                )
            )
        yr[a, pl.ds(g_me[a], 1), :, :w] = ys[a, pl.ds(g_me[a], 1), :, :w]

    lik = jnp.zeros((GRP, width), F32)
    group_loglik = jnp.zeros((GRP, LANES), F32)
    for a in range(2):
        for copy in y_c[a]:
            copy.wait_recv()
        part = yr[a, :, :, :half_w].reshape(NY * GRP, half_w)
        back = dot(part, perm[:, a * half_w : (a + 1) * half_w], ((1,), (1,)))
        for g in range(NY):
            lik = lik + back[g * GRP : (g + 1) * GRP, :]
        if a == 0:
            for g in range(NY):
                group_loglik = group_loglik + yr[a, g, :, half_w:].astype(F32)

    offset = new_pos[...] - pm[...]
    grad_now = lik + pp[...] * offset
    mom_now = half_s[...] - 0.5 * step_size * grad_now
    new_grd[...] = grad_now
    new_mom[...] = mom_now
    quad = 0.5 * (pp[...] * offset * offset + im[...] * mom_now * mom_now)
    total = quad[:, :LANES]
    for b in range(1, width // LANES):
        total = total + quad[:, b * LANES : (b + 1) * LANES]
    shift = LANES // 2
    while shift >= CHAINS:
        total = total + pltpu.roll(total, shift, 1)
        shift //= 2
    total = total + group_loglik + pltpu.roll(group_loglik, LANES - CHAINS, 1)
    er[pl.ds(k, 1)] = total[None]
    e_c = []
    for i in x_order:
        e_c.append(send(er.at[k], er.at[k], e_ss.at[i], e_rs.at[i], xpeer(i)))
    for copy in e_c:
        copy.wait_recv()
    whole = er[0]
    for kk in range(1, nf):
        whole = whole + er[kk]
    energy[...] = whole[:, :CHAINS]
    for copy in copies:
        copy.wait_send()


def body(observations, labels, tile_live, tile_group, position, momentum, gradient, prior_mean, prior_prec, inv_mass):
    tiles, quarter, row_count = observations.shape
    groups, width = position.shape
    chains = width // quarter
    nf = lax.axis_size("feat")
    half_w = width // 2
    share = tiles // nf
    S = NY * NC
    prior_full = jnp.repeat(prior_prec, chains)[None, :]
    mass_full = jnp.repeat(inv_mass, chains)[None, :]
    V = pltpu.VMEM
    D = pltpu.SemaphoreType.DMA
    scratch = [
        V((share, nf * quarter, row_count), BF),
        V((width, width), BF),
        V((share, row_count), F32),
        V((tiles, LANES), F32),
        V((groups, width), F32),
        V((tiles, LANES), BF),
        V((2, NY, GRP, half_w), BF),
        V((2, S, 2 * NY, LANES), BF),
        V((2, S, 2 * NY, LANES), BF),
        V((2, tiles, S * 2 * NY), BF),
        V((2, S * 2 * NY, tiles), BF),
        V((2, S * 2 * NY, LANES), BF),
        V((2, LANES, S * 2 * NY), BF),
        V((2, S, 2 * NY, half_w), BF),
        V((2, S, 2 * NY, half_w), BF),
        V((2, nf, share, half_w), BF),
        V((2, nf, share, half_w), BF),
        V((2, nf, share, half_w), BF),
        V((2, nf, share, half_w), BF),
        V((CHAINS * share, LANES), F32),
        V((CHAINS * share, LANES), F32),
        V((2, S, 2 * NY, half_w + LANES), BF),
        V((2, S, 2 * NY, half_w + LANES), BF),
        V((2, NY, GRP, half_w + LANES), BF),
        V((2, NY, GRP, half_w + LANES), BF),
        V((nf, groups, LANES), F32),
        D((nf,)),
        D((nf,)),
        D(()),
        D((2, NY)),
        D((2, NY)),
        D((2, S)),
        D((2, S)),
        D((2, S)),
        D((2, S)),
        D((2, nf)),
        D((2, nf)),
        D((2, nf)),
        D((2, nf)),
        D((2, S)),
        D((2, S)),
        D((2, NY)),
        D((2, NY)),
        D((nf,)),
        D((nf,)),
    ]
    vm = pl.BlockSpec(memory_space=pltpu.VMEM)
    moved, new_mom, new_grd, energy = pl.pallas_call(
        kernel,
        out_shape=(
            jax.ShapeDtypeStruct((groups, width), F32),
            jax.ShapeDtypeStruct((groups, width), F32),
            jax.ShapeDtypeStruct((groups, width), F32),
            jax.ShapeDtypeStruct((groups, chains), F32),
        ),
        in_specs=[pl.BlockSpec(memory_space=pl.ANY)] + [vm] * 9,
        out_specs=(vm, vm, vm, vm),
        scratch_shapes=scratch,
        compiler_params=pltpu.CompilerParams(collective_id=0, has_side_effects=True),
        name="leapfrog",
    )(
        observations,
        labels,
        tile_live[None, :],
        tile_group[None, :],
        position,
        momentum,
        gradient,
        prior_mean[None, :],
        prior_full,
        mass_full,
    )
    return moved, new_mom, new_grd, energy


def solution(mesh):
    placed = (
        P("dp", "feat", None),
        P("dp", None),
        P("dp"),
        P("dp"),
        P("dp", "feat"),
        P("dp", "feat"),
        P("dp", "feat"),
        P("feat"),
        P("feat"),
        P("feat"),
    )
    return jax.shard_map(
        body,
        mesh=mesh,
        in_specs=placed,
        out_specs=(P("dp", "feat"), P("dp", "feat"), P("dp", "feat"), P("dp", None)),
        check_vma=False,
    )
```

time: 127 us -> 62 us (0.49); the launches traced: 124 us -> 61.6 us
  Pallas kernels: 0 us -> 55.4 us
  waiting for transfers between devices: 51.7 us -> 0 us
  starting transfers between devices: 42.5 us -> 0 us
  local copies, waits for them, and re-layouts: 13.7 us -> 5.58 us
  blocking collectives: 7.54 us -> 0 us
  other arithmetic: 4.6 us -> 0 us
  matrix products: 3.07 us -> 0 us
    pallas_call x0 -> x1, Pallas kernels: none -> 55.4 us  [body(): pl.pallas_call(kernel, out_shape=(jax.ShapeDtypeStruct((groups, width), F...]
    all_to_all x5 -> x0, waiting for transfers between devices: 51.7 us -> none  [the longest x1 15.2 us: sent_together(): lax.all_to_all(both, axis, split_axis=split_dim, concat_axis=concat_dim,...]
    all_to_all x5 -> x0, starting transfers between devices: 42.5 us -> none  [the longest x1 18.5 us: body(): lax.all_to_all(requests, 'dp', split_axis=0, concat_axis=0, tiled=True)]
    psum x1 -> x0, blocking collectives: 7.54 us -> none  [body(): energy = lax.psum(summed, 'feat')]
    gather x6 -> x0, local copies, waits for them, and re-layouts: 4.95 us -> none  [the longest x1 1.87 us: body(): tile_group[safe_tile]]
    dot_general x5 -> x0, matrix products: 3.07 us -> none  [the longest x1 1.22 us: body(): jnp.einsum('tfc,tfr->tcr', tile_coeffs, observations, preferred_element_t...]
    unnamed x20 -> x14, local copies, waits for them, and re-layouts: 2.31 us -> 4.11 us
    convert_element_type x4 -> x0, other arithmetic: 1.57 us -> none  [the longest x1 0.72 us: likelihood(): targets = labels.astype(jnp.float32)[:, None, :]]
  transfers between devices with their start and end apart: 5 -> 0, of which waited for: 5 -> 0; matrix products, arithmetic and copies ran while one was open for 2% -> 0% of each run, Pallas kernels for 0% -> 0%
where the time goes in v1:
time: 62 us; the launch traced here: 61.6 us
  Pallas kernels  55.4 us (89%)
  local copies, waits for them, and re-layouts  5.58 us (9%)
  between operations  0.66 us (1%)
    pallas_call x1, Pallas kernels, body(): pl.pallas_call(kernel, out_shape=(jax.ShapeDtypeStruct((groups, width), F...  55.4 us
    unnamed x14, local copies, waits for them, and re-layouts  4.11 us

profile of v1, /device:TPU:1, one launch (start us, length us, event | category | flops | bytes accessed | tf_op | source)
XLA Modules:
  0.0 61.6 jit_solution(2253832864265000829)
XLA Ops:
  0.6 0.0 copy-start.3
  0.6 0.6 %copy-done.3 = f32[32]{0:T(128)S(1)} copy-done((f32[32]{0:T(128)S(1)}, f32[32]{0:T(128)}, u32[]{:S(2)}) %copy-start.3) | copy-done | bytes 152
  1.3 0.1 broadcast_in_dim.18
  1.4 0.0 copy-start.4
  1.4 0.7 %broadcast_in_dim_reshape.6.pp = f32[1,512]{1,0:T(1,128)} reshape(f32[32,16]{1,0:T(8,128)S(1)} %broadcast_in_dim.18) | data formatting | bytes 4096 | tf_op jit(solution)/shard_map/broadcast_in_dim;reshape | solution.py:417
  2.0 0.0 copy-done.4
  2.0 0.1 broadcast_in_dim.19
  2.1 0.7 %broadcast_in_dim_reshape.7.im = f32[1,512]{1,0:T(1,128)} reshape(f32[32,16]{1,0:T(8,128)S(1)} %broadcast_in_dim.19) | data formatting | bytes 4096 | tf_op jit(solution)/shard_map/broadcast_in_dim;reshape | solution.py:418
  2.8 55.4 %leapfrog.1 = (f32[16,512]{1,0:T(8,128)}, f32[16,512]{1,0:T(8,128)}, f32[16,512]{1,0:T(8,128)}, f32[16,16]{1,0:T(8,128)}) custom-call(bf16[128,32,128]{2,1,0:T(8,128)(2,1)} %obs.1, s32[128,128]{1,0:T(8,128)} %lab.1, s32[1,128]{1,0:T(1,128)} %bitcast.4, s32[1,128]{1,0:T(1,128)} %bitcast.5, f32[16,512]{1,0:T(8,128)} %pos.1, f32[16,512]{1,0:T(8,128)} %mom.1, ...), custom_call_target="tpu_custom_call" | custom-call | tf_op jit(solution)/shard_map/leapfrog/pallas_call | solution.py:469
  58.2 0.0 copy-start.1
  58.2 1.4 %copy.18 = f32[16,512]{1,0:T(8,128)} copy(f32[16,512]{1,0:T(8,128)} %get-tuple-element.8) | data formatting | bytes 65536
  59.6 0.0 copy-done.1
  59.6 0.0 copy-start
  59.6 0.6 copy.19
  60.2 0.2 copy-done
  60.3 0.0 copy-start.2
  60.3 0.6 copy.20
  60.9 0.1 copy-done.2
  61.0 0.6 copy.21
Async XLA Ops:
  0.6 0.7 %copy-start.3 = (f32[32]{0:T(128)S(1)}, f32[32]{0:T(128)}, u32[]{:S(2)}) copy-start(f32[32]{0:T(128)} %param.18) | copy-start | bytes 388
  1.4 0.7 %copy-start.4 = (f32[32]{0:T(128)S(1)}, f32[32]{0:T(128)}, u32[]{:S(2)}) copy-start(f32[32]{0:T(128)} %param.19) | copy-start | bytes 388
  58.2 1.4 %copy-start.1 = (f32[16,512]{1,0:T(8,128)S(1)}, f32[16,512]{1,0:T(8,128)}, u32[]{:S(2)}) copy-start(f32[16,512]{1,0:T(8,128)} %get-tuple-element.9) | copy-start | bytes 98308
  59.6 0.8 %copy-start = (f32[16,512]{1,0:T(8,128)S(1)}, f32[16,512]{1,0:T(8,128)}, u32[]{:S(2)}) copy-start(f32[16,512]{1,0:T(8,128)} %get-tuple-element.10) | copy-start | bytes 98308
  60.3 0.7 %copy-start.2 = (f32[16,16]{1,0:T(8,128)S(1)}, f32[16,16]{1,0:T(8,128)}, u32[]{:S(2)}) copy-start(f32[16,16]{1,0:T(8,128)} %get-tuple-element.11) | copy-start | bytes 3076

commit v2 on v1

--- a/solution.py
+++ b/solution.py
@@ -33,6 +33,19 @@
 
 def kernel(
     obs,
+    lab_h,
+    live_h,
+    tg_h,
+    pos_h,
+    mom_h,
+    grd_h,
+    pm_h,
+    pp_h,
+    im_h,
+    new_pos,
+    new_mom,
+    new_grd,
+    energy,
     lab,
     live,
     tg,
@@ -40,12 +53,9 @@
     mom,
     grd,
     pm,
-    pp,
-    im,
-    new_pos,
-    new_mom,
-    new_grd,
-    energy,
+    ppim_p,
+    ppim_m,
+    in_s,
     obsx,
     perm,
     labf,
@@ -55,6 +65,7 @@
     gat,
     rqs,
     rq,
+    fold,
     tmat,
     tmat_t,
     smat,
@@ -67,6 +78,8 @@
     gr,
     wf,
     gf,
+    lg,
+    res,
     ms,
     mr,
     ys,
@@ -95,10 +108,10 @@
     d = lax.axis_index("dp")
     k = lax.axis_index("feat")
     y, z, c = d // (NY * NC), (d // NC) % NY, d % NC
-    tiles = lab.shape[0]
+    tiles = lab_h.shape[0]
     nf = 4
     share = tiles // nf
-    width = pos.shape[1]
+    width = pos_h.shape[1]
     quarter = width // CHAINS
     half_w = width // 2
 
@@ -138,20 +151,54 @@
                 pl.semaphore_signal(barrier, inc=1, device_id=who, device_id_type=MESH)
                 count += 1
 
+    loads = []
+    for i, (far, near) in enumerate(
+        (
+            (tg_h, tg),
+            (pp_h, ppim_p),
+            (im_h, ppim_m),
+            (pos_h, pos),
+            (mom_h, mom),
+            (grd_h, grd),
+            (pm_h, pm),
+            (live_h, live),
+            (lab_h, lab),
+        )
+    ):
+        loads.append(pltpu.make_async_copy(far, near, in_s.at[i]))
+        loads[-1].start()
+
     src = lax.broadcasted_iota(jnp.int32, (LANES, width), 0)
     dst = lax.broadcasted_iota(jnp.int32, (LANES, width), 1)
     want = (dst % quarter) * CHAINS + dst // quarter
     for b in range(width // LANES):
         perm[b * LANES : (b + 1) * LANES, :] = one_hot(src + b * LANES == want)
 
+    for copy in loads[1:7]:
+        copy.wait()
+    row8 = lax.broadcasted_iota(jnp.int32, (8, quarter), 0)
+    pieces = jnp.zeros((8, quarter), F32)
+    for n, ref in enumerate((ppim_p, ppim_m)):
+        rest = ref[...]
+        for m in range(3):
+            piece = rest.astype(BF).astype(F32)
+            pieces = jnp.where(row8 == 3 * n + m, piece, pieces)
+            rest = rest - piece
+    feature = lax.broadcasted_iota(jnp.int32, (quarter, width), 0)
+    chain_lane = lax.broadcasted_iota(jnp.int32, (quarter, width), 1)
+    spread = dot(pieces.astype(BF), one_hot(chain_lane // CHAINS == feature))
+    pp = (spread[0:1, :] + spread[1:2, :]) + spread[2:3, :]
+    im = (spread[3:4, :] + spread[4:5, :]) + spread[5:6, :]
+
     half = mom[...] - 0.5 * step_size * grd[...]
-    moved = pos[...] + step_size * im[...] * half
+    moved = pos[...] + step_size * im * half
     half_s[...] = half
     new_pos[...] = moved
     block = dot(moved.astype(BF), perm[...]).astype(BF)
     for a in range(2):
         gat[a, pl.ds(g_me[a], 1)] = block[None, :, a * half_w : (a + 1) * half_w]
 
+    loads[0].wait()
     tile_row = jnp.broadcast_to(tg[...], (tiles, tiles))
     tile_col = jnp.transpose(tile_row.astype(F32)).astype(jnp.int32)
     own_row, own_col = tile_row // GRP, tile_col // GRP
@@ -170,13 +217,13 @@
         return (second * NC + oc) * (NY * 2) + first * 2 + rank, first
 
     for a in range(2):
-        s_r, _ = slot_of(a, own_row, rank_row)
-        s_c, first = slot_of(a, own_col, rank_col)
-        asked = (first * GRP + tile_col % GRP + 1).astype(F32).astype(BF)
+        s_r, first = slot_of(a, own_row, rank_row)
+        asked = (first * GRP + tile_row % GRP + 1)[:16, :].astype(F32).astype(BF)
+        s_c, _ = slot_of(a, own_col, rank_col)
         for b in range(slots // LANES):
             tmat[a, :, b * LANES : (b + 1) * LANES] = one_hot(s_c == t_row + b * LANES)
             tmat_t[a, b * LANES : (b + 1) * LANES, :] = one_hot(s_r == t_col + b * LANES)
-        rqs[a] = dot(tmat_t[a], asked).astype(BF).reshape(NY * NC, NY * 2, LANES)
+        rqs[a] = dot(asked, tmat[a])[:1, :]
 
     pl.semaphore_wait(barrier, count)
 
@@ -193,13 +240,12 @@
     gat_c = [[], []]
     rq_c = [[], []]
     for a in range(2):
+        for i in s_order:
+            rq_c[a].append(send(rqs.at[a], rq.at[a, s_me[a]], rq_ss.at[a, i], rq_rs.at[a, i], s_peer(a, i)))
+    for a in range(2):
         for i in g_order:
             ref = gat.at[a, g_me[a]]
             gat_c[a].append(send(ref, ref, gat_ss.at[a, i], gat_rs.at[a, i], g_peer(a, i)))
-    for a in range(2):
-        for i in s_order:
-            q = (s_me[a] + i) % (NY * NC)
-            rq_c[a].append(send(rqs.at[a, q], rq.at[a, s_me[a]], rq_ss.at[a, i], rq_rs.at[a, i], s_peer(a, i)))
     obs_c = []
     for i in x_order:
         to = (k + i) % nf
@@ -219,24 +265,32 @@
     )
     own_copy.start()
 
+    loads[7].wait()
+    loads[8].wait()
     rows = pl.ds(pl.multiple_of(k * share, share), share)
     labf[...] = lab[rows, :].astype(F32)
     live_col = jnp.transpose(jnp.broadcast_to(live[...], (tiles, tiles)).astype(F32))
     mask[...] = jnp.where(t_row.astype(F32) < live_col, 1.0, 0.0)
     ltile[...] = jnp.zeros_like(ltile)
-
-    for a in range(2):
-        rq[a, pl.ds(s_me[a], 1)] = rqs[a, pl.ds(s_me[a], 1)]
+    for b in range(slots // LANES):
+        here = lax.broadcasted_iota(jnp.int32, (LANES, slots), 0) + b * LANES
+        there = lax.broadcasted_iota(jnp.int32, (LANES, slots), 1)
+        fold[b * LANES : (b + 1) * LANES, :] = one_hot(here % (NY * 2) == there % (NY * 2))
+
+    lane_q = lax.broadcasted_iota(jnp.int32, (NY * NC, slots), 1) // (NY * 2)
+    row_q = lax.broadcasted_iota(jnp.int32, (NY * NC, slots), 0)
+    for a in range(2):
+        rq[a, pl.ds(s_me[a], 1)] = rqs[a][None]
         for copy in rq_c[a]:
             copy.wait_recv()
-        ask = rq[a].reshape(slots, LANES).astype(F32)
-        lane1 = (lax.broadcasted_iota(jnp.int32, (slots, LANES), 1) + 1).astype(F32)
-        chosen = jnp.where(ask == lane1, 1.0, 0.0)
-        smat[a] = chosen.astype(BF)
+        asks = jnp.where(lane_q == s_me[a], rq[a].reshape(NY * NC, slots), 0.0).astype(BF)
+        asks = jnp.where(lane_q == row_q, dot(asks, fold[...]), 0.0)
+        ask = jnp.sum(asks, axis=0, keepdims=True)
         for b in range(slots // LANES):
-            smat_t[a, :, b * LANES : (b + 1) * LANES] = jnp.transpose(
-                chosen[b * LANES : (b + 1) * LANES, :]
-            ).astype(BF)
+            part = jnp.broadcast_to(ask[:, b * LANES : (b + 1) * LANES], (LANES, LANES))
+            chosen = jnp.where(part == (t_col + 1).astype(F32), 1.0, 0.0)
+            smat_t[a, :, b * LANES : (b + 1) * LANES] = chosen.astype(BF)
+            smat[a, b * LANES : (b + 1) * LANES, :] = jnp.transpose(chosen).astype(BF)
 
     sel_c = [[], []]
     for a in range(2):
@@ -287,18 +341,20 @@
     base = k * share
     for t in range(share):
         coeff = wf[pl.ds(t, CHAINS, stride=share), :].astype(BF)
-        tile = obsx[t]
-        logits = dot(coeff, tile)
+        lg[t * CHAINS : (t + 1) * CHAINS, :] = dot(coeff, obsx[t])
+    for t in range(share):
+        logits = lg[t * CHAINS : (t + 1) * CHAINS, :]
         target = jnp.broadcast_to(labf[t : t + 1, :], (CHAINS, LANES))
         alive = jnp.broadcast_to(mask[pl.ds(base + t, 1), :], (CHAINS, LANES)) > 0.5
         e = jnp.exp(-jnp.abs(logits))
         r = 1.0 / (1.0 + e)
         sig = jnp.where(logits >= 0.0, r, e * r)
-        residual = jnp.where(alive, sig - target, 0.0).astype(BF)
+        res[t * CHAINS : (t + 1) * CHAINS, :] = jnp.where(alive, sig - target, 0.0).astype(BF)
         soft = jnp.maximum(logits, 0.0) + jnp.log1p(e)
         term = jnp.where(alive, soft - target * logits, 0.0)
         loglik = jnp.where(lane16 == t, jnp.sum(term, axis=1, keepdims=True), loglik)
-        gf[pl.ds(t, CHAINS, stride=share), :] = dot(residual, tile, ((1,), (1,)))
+    for t in range(share):
+        gf[pl.ds(t, CHAINS, stride=share), :] = dot(res[t * CHAINS : (t + 1) * CHAINS, :], obsx[t], ((1,), (1,)))
 
     gx_c = [[], []]
     for a in range(2):
@@ -379,11 +435,11 @@
                 group_loglik = group_loglik + yr[a, g, :, half_w:].astype(F32)
 
     offset = new_pos[...] - pm[...]
-    grad_now = lik + pp[...] * offset
+    grad_now = lik + pp * offset
     mom_now = half_s[...] - 0.5 * step_size * grad_now
     new_grd[...] = grad_now
     new_mom[...] = mom_now
-    quad = 0.5 * (pp[...] * offset * offset + im[...] * mom_now * mom_now)
+    quad = 0.5 * (pp * offset * offset + im * mom_now * mom_now)
     total = quad[:, :LANES]
     for b in range(1, width // LANES):
         total = total + quad[:, b * LANES : (b + 1) * LANES]
@@ -406,6 +462,13 @@
         copy.wait_send()
 
 
+def hand_over(a, b, c, d, a_out, b_out, c_out, d_out):
+    a_out[...] = a[...]
+    b_out[...] = b[...]
+    c_out[...] = c[...]
+    d_out[...] = d[...]
+
+
 def body(observations, labels, tile_live, tile_group, position, momentum, gradient, prior_mean, prior_prec, inv_mass):
     tiles, quarter, row_count = observations.shape
     groups, width = position.shape
@@ -414,11 +477,20 @@
     half_w = width // 2
     share = tiles // nf
     S = NY * NC
-    prior_full = jnp.repeat(prior_prec, chains)[None, :]
-    mass_full = jnp.repeat(inv_mass, chains)[None, :]
     V = pltpu.VMEM
     D = pltpu.SemaphoreType.DMA
+    S = NY * NC
     scratch = [
+        V((tiles, row_count), jnp.int32),
+        V((1, tiles), jnp.int32),
+        V((1, tiles), jnp.int32),
+        V((groups, width), F32),
+        V((groups, width), F32),
+        V((groups, width), F32),
+        V((1, width), F32),
+        V((1, quarter), F32),
+        V((1, quarter), F32),
+        D((9,)),
         V((share, nf * quarter, row_count), BF),
         V((width, width), BF),
         V((share, row_count), F32),
@@ -426,8 +498,9 @@
         V((groups, width), F32),
         V((tiles, LANES), BF),
         V((2, NY, GRP, half_w), BF),
-        V((2, S, 2 * NY, LANES), BF),
-        V((2, S, 2 * NY, LANES), BF),
+        V((2, 1, S * 2 * NY), F32),
+        V((2, S, 1, S * 2 * NY), F32),
+        V((S * 2 * NY, S * 2 * NY), BF),
         V((2, tiles, S * 2 * NY), BF),
         V((2, S * 2 * NY, tiles), BF),
         V((2, S * 2 * NY, LANES), BF),
@@ -440,6 +513,8 @@
         V((2, nf, share, half_w), BF),
         V((CHAINS * share, LANES), F32),
         V((CHAINS * share, LANES), F32),
+        V((CHAINS * share, LANES), F32),
+        V((CHAINS * share, LANES), BF),
         V((2, S, 2 * NY, half_w + LANES), BF),
         V((2, S, 2 * NY, half_w + LANES), BF),
         V((2, NY, GRP, half_w + LANES), BF),
@@ -466,15 +541,16 @@
         D((nf,)),
     ]
     vm = pl.BlockSpec(memory_space=pltpu.VMEM)
-    moved, new_mom, new_grd, energy = pl.pallas_call(
+    shapes = (
+        jax.ShapeDtypeStruct((groups, width), F32),
+        jax.ShapeDtypeStruct((groups, width), F32),
+        jax.ShapeDtypeStruct((groups, width), F32),
+        jax.ShapeDtypeStruct((groups, chains), F32),
+    )
+    results = pl.pallas_call(
         kernel,
-        out_shape=(
-            jax.ShapeDtypeStruct((groups, width), F32),
-            jax.ShapeDtypeStruct((groups, width), F32),
-            jax.ShapeDtypeStruct((groups, width), F32),
-            jax.ShapeDtypeStruct((groups, chains), F32),
-        ),
-        in_specs=[pl.BlockSpec(memory_space=pl.ANY)] + [vm] * 9,
+        out_shape=shapes,
+        in_specs=[pl.BlockSpec(memory_space=pltpu.HBM)] * 10,
         out_specs=(vm, vm, vm, vm),
         scratch_shapes=scratch,
         compiler_params=pltpu.CompilerParams(collective_id=0, has_side_effects=True),
@@ -488,10 +564,16 @@
         momentum,
         gradient,
         prior_mean[None, :],
-        prior_full,
-        mass_full,
+        prior_prec[None, :],
+        inv_mass[None, :],
     )
-    return moved, new_mom, new_grd, energy
+    return pl.pallas_call(
+        hand_over,
+        out_shape=shapes,
+        in_specs=[vm] * 4,
+        out_specs=(vm, vm, vm, vm),
+        name="hand_over",
+    )(*results)
 
 
 def solution(mesh):

time: 62 us -> 55.2 us (0.89)
  local copies, waits for them, and re-layouts: 5.58 us -> 0 us
  Pallas kernels: 55.4 us -> 54.1 us
    unnamed x14 -> x0, local copies, waits for them, and re-layouts: 4.11 us -> none
    another operation x2 -> x0, local copies, waits for them, and re-layouts: 1.32 us -> none  [the longest x1 0.66 us: body(): mass_full = jnp.repeat(inv_mass, chains)[None, :]]
    pallas_call x1 -> x2, Pallas kernels: 55.4 us -> 54.1 us  [the longest x1 52.7 us: body(): pl.pallas_call(kernel, out_shape=shapes, in_specs=[pl.BlockSpec(memory_sp...]
where the time goes in v2:
time: 55.2 us; the launch traced here: 54.8 us
  Pallas kernels  54.1 us (98%)
  between operations  0.64 us (1%)
    pallas_call x1, Pallas kernels, body(): pl.pallas_call(kernel, out_shape=shapes, in_specs=[pl.BlockSpec(memory_sp...  52.7 us
    pallas_call x1, Pallas kernels, body(): pl.pallas_call(hand_over, out_shape=shapes, in_specs=[vm] * 4, out_specs=...  1.44 us

profile of v2, /device:TPU:1, one launch (start us, length us, event | category | flops | bytes accessed | tf_op | source)
XLA Modules:
  0.0 54.8 jit_solution(13955019476983939489)
XLA Ops:
  0.6 52.7 %leapfrog.1 = (f32[16,512]{1,0:T(8,128)}, f32[16,512]{1,0:T(8,128)}, f32[16,512]{1,0:T(8,128)}, f32[16,16]{1,0:T(8,128)}) custom-call(bf16[128,32,128]{2,1,0:T(8,128)(2,1)} %obs.1, s32[128,128]{1,0:T(8,128)} %lab_h.1, s32[1,128]{1,0:T(1,128)} %bitcast.6, s32[1,128]{1,0:T(1,128)} %bitcast.7, f32[16,512]{1,0:T(8,128)} %pos_h.1, f32[16,512]{1,0:T(8,128)} %mom_h.1, ...), custom_call_target="tpu_custom_call" | custom-call | tf_op jit(solution)/shard_map/leapfrog/pallas_call | solution.py:550
  53.4 1.4 %hand_over.1 = (f32[16,512]{1,0:T(8,128)}, f32[16,512]{1,0:T(8,128)}, f32[16,512]{1,0:T(8,128)}, f32[16,16]{1,0:T(8,128)}) custom-call(f32[16,512]{1,0:T(8,128)} %get-tuple-element.8.a, f32[16,512]{1,0:T(8,128)} %get-tuple-element.9.b, f32[16,512]{1,0:T(8,128)} %get-tuple-element.10.c, f32[16,16]{1,0:T(8,128)} %get-tuple-element.11.d), custom_call_target="tpu_custom_call" | custom-call | tf_op jit(solution)/shard_map/hand_over/pallas_call | solution.py:570

commit v3 on v2

v3 whole, which is shorter than its diff:
```python
import functools

import jax
import jax.numpy as jnp
from jax import lax
from jax.experimental import pallas as pl
from jax.experimental.pallas import tpu as pltpu
from jax.sharding import PartitionSpec as P

MESH = pl.DeviceIdType.MESH
step_size = 0.1

NY = 8
NC = 2
CHAINS = 16
HALVES = 1
GRP = 16
LANES = 128
BF = jnp.bfloat16
F32 = jnp.float32


def far_first(n):
    return sorted(range(1, n), key=lambda i: -min(i, n - i))


def dot(a, b, contract=((1,), (0,))):
    return lax.dot_general(a, b, (contract, ((), ())), preferred_element_type=F32)


def one_hot(flags):
    return jnp.where(flags, 1.0, 0.0).astype(BF)


def kernel(
    obs,
    lab_h,
    live_h,
    tg_h,
    pos_h,
    mom_h,
    grd_h,
    pm_h,
    pp_h,
    im_h,
    new_pos,
    new_mom,
    new_grd,
    energy,
    lab,
    live,
    tg,
    pos,
    mom,
    grd,
    pm,
    ppim_p,
    ppim_m,
    in_s,
    obs_v,
    obsx,
    perm,
    labf,
    mask,
    half_s,
    ltile,
    gat,
    rqs,
    rq,
    fold,
    tmat,
    tmat_t,
    smat,
    smat_t,
    sels,
    selr,
    xs,
    xr,
    gs,
    gr,
    wf,
    gf,
    lg,
    res,
    ms,
    mr,
    ls,
    lr,
    zs,
    zr,
    ys,
    yr,
    er,
    obs_ss,
    obs_rs,
    own_s,
    gat_ss,
    gat_rs,
    rq_ss,
    rq_rs,
    sel_ss,
    sel_rs,
    x_ss,
    x_rs,
    gx_ss,
    gx_rs,
    m_ss,
    m_rs,
    l_ss,
    l_rs,
    z_ss,
    z_rs,
    y_ss,
    y_rs,
    e_ss,
    e_rs,
):
    d = lax.axis_index("dp")
    k = lax.axis_index("feat")
    y, z, c = d // (NY * NC), (d // NC) % NY, d % NC
    tiles = lab_h.shape[0]
    nf = 4
    share = tiles // nf
    part_t = share // HALVES
    width = pos_h.shape[1]
    quarter = width // CHAINS
    half_w = width // 2

    def at(yy, zz, cc):
        return ((yy * NY + zz) * NC + cc, k)

    def xpeer(i):
        return (d, (k + i) % nf)

    g_me = (y, z)
    s_me = (z * NC + c, y * NC + c)

    def g_peer(a, i):
        return at((y + i) % NY, z, c) if a == 0 else at(y, (z + i) % NY, c)

    def s_peer(a, i):
        q = (s_me[a] + i) % (NY * NC)
        return at(y, q // NC, q % NC) if a == 0 else at(q // NC, z, q % NC)

    x_order = (2, 1, 3)
    g_order = far_first(NY)
    s_order = far_first(NY * NC)

    barrier = pltpu.get_barrier_semaphore()
    greet = []
    for i in g_order:
        greet += [g_peer(0, i), g_peer(1, i)]
    for i in g_order:
        greet += [at((y + i) % NY, z, 1 - c), at(y, (z + i) % NY, 1 - c)]
    greet += [xpeer(i) for i in x_order] + [at(y, z, 1 - c)]
    for who in greet:
        pl.semaphore_signal(barrier, inc=1, device_id=who, device_id_type=MESH)
    count = len(greet)

    loads = []
    for i, (far, near) in enumerate(
        (
            (tg_h, tg),
            (pp_h, ppim_p),
            (im_h, ppim_m),
            (pos_h, pos),
            (mom_h, mom),
            (grd_h, grd),
            (pm_h, pm),
            (live_h, live),
            (lab_h, lab),
            (obs, obs_v),
        )
    ):
        loads.append(pltpu.make_async_copy(far, near, in_s.at[i]))
        loads[-1].start()

    src = lax.broadcasted_iota(jnp.int32, (LANES, width), 0)
    dst = lax.broadcasted_iota(jnp.int32, (LANES, width), 1)
    want = (dst % quarter) * CHAINS + dst // quarter
    for b in range(width // LANES):
        perm[b * LANES : (b + 1) * LANES, :] = one_hot(src + b * LANES == want)

    for copy in loads[1:7]:
        copy.wait()
    row8 = lax.broadcasted_iota(jnp.int32, (8, quarter), 0)
    pieces = jnp.zeros((8, quarter), F32)
    for n, ref in enumerate((ppim_p, ppim_m)):
        rest = ref[...]
        for m in range(3):
            piece = rest.astype(BF).astype(F32)
            pieces = jnp.where(row8 == 3 * n + m, piece, pieces)
            rest = rest - piece
    feature = lax.broadcasted_iota(jnp.int32, (quarter, width), 0)
    chain_lane = lax.broadcasted_iota(jnp.int32, (quarter, width), 1)
    spread = dot(pieces.astype(BF), one_hot(chain_lane // CHAINS == feature))
    pp = (spread[0:1, :] + spread[1:2, :]) + spread[2:3, :]
    im = (spread[3:4, :] + spread[4:5, :]) + spread[5:6, :]

    half = mom[...] - 0.5 * step_size * grd[...]
    moved = pos[...] + step_size * im * half
    half_s[...] = half
    new_pos[...] = moved
    block = dot(moved.astype(BF), perm[...]).astype(BF)
    for a in range(2):
        gat[a, pl.ds(g_me[a], 1)] = block[None, :, a * half_w : (a + 1) * half_w]

    loads[0].wait()
    tile_row = jnp.broadcast_to(tg[...], (tiles, tiles))
    tile_col = jnp.transpose(tile_row.astype(F32)).astype(jnp.int32)
    own_row, own_col = tile_row // GRP, tile_col // GRP
    t_row = lax.broadcasted_iota(jnp.int32, (tiles, tiles), 1)
    t_col = lax.broadcasted_iota(jnp.int32, (tiles, tiles), 0)
    same = own_row == own_col
    rank_row = jnp.sum(jnp.where(same & (t_col < t_row), 1.0, 0.0), axis=0, keepdims=True)
    rank_row = jnp.broadcast_to(rank_row, (tiles, tiles))
    rank_col = jnp.transpose(rank_row).astype(jnp.int32)
    rank_row = rank_row.astype(jnp.int32)
    slots = NY * NC * NY * 2

    def slot_of(a, own, rank):
        oy, oz, oc = own // (NY * NC), (own // NC) % NY, own % NC
        first, second = (oy, oz) if a == 0 else (oz, oy)
        return (second * NC + oc) * (NY * 2) + first * 2 + rank, first

    for b in range(slots // LANES):
        here = lax.broadcasted_iota(jnp.int32, (LANES, slots), 0) + b * LANES
        there = lax.broadcasted_iota(jnp.int32, (LANES, slots), 1)
        fold[b * LANES : (b + 1) * LANES, :] = one_hot(here % (NY * 2) == there % (NY * 2))
    lane_q = lax.broadcasted_iota(jnp.int32, (NY * NC, slots), 1) // (NY * 2)
    row_q = lax.broadcasted_iota(jnp.int32, (NY * NC, slots), 0)
    for a in range(2):
        s_r, first = slot_of(a, own_row, rank_row)
        asked = (first * GRP + tile_row % GRP + 1)[:16, :].astype(F32).astype(BF)
        s_c, _ = slot_of(a, own_col, rank_col)
        for b in range(slots // LANES):
            tmat[a, :, b * LANES : (b + 1) * LANES] = one_hot(s_c == t_row + b * LANES)
            tmat_t[a, b * LANES : (b + 1) * LANES, :] = one_hot(s_r == t_col + b * LANES)
        wanted = jnp.broadcast_to(dot(asked, tmat[a])[:1, :], (NY * NC, slots))
        spread_q = dot(jnp.where(lane_q == row_q, wanted, 0.0).astype(BF), fold[...])
        placed = jnp.where(lane_q == s_me[a], spread_q, 0.0)
        for q in range(NY * NC):
            rqs[a, q] = placed[q : q + 1, :]

    pl.semaphore_wait(barrier, count)

    copies = []

    def send(src_ref, dst_ref, ss, rs, who):
        copy = pltpu.make_async_remote_copy(
            src_ref=src_ref, dst_ref=dst_ref, send_sem=ss, recv_sem=rs, device_id=who, device_id_type=MESH
        )
        copy.start()
        copies.append(copy)
        return copy

    gat_c = [[], []]
    rq_c = [[], []]
    hops = {}
    for i in s_order:
        hops.setdefault(min(i // NC, NY - i // NC), []).append(i)
    for far in sorted(hops, reverse=True):
        for i in hops[far]:
            for a in range(2):
                q = (s_me[a] + i) % (NY * NC)
                rq_c[a].append(
                    send(rqs.at[a, q], rq.at[a, s_me[a]], rq_ss.at[a, i], rq_rs.at[a, i], s_peer(a, i))
                )
        for i in g_order:
            if min(i, NY - i) == far:
                for a in range(2):
                    ref = gat.at[a, g_me[a]]
                    gat_c[a].append(send(ref, ref, gat_ss.at[a, i], gat_rs.at[a, i], g_peer(a, i)))
    loads[9].wait()
    obs_c = []
    for i in x_order:
        to = (k + i) % nf
        obs_c.append(
            send(
                obs_v.at[pl.ds(to * share, share)],
                obsx.at[:, pl.ds(pl.multiple_of(k * quarter, quarter), quarter), :],
                obs_ss.at[i],
                obs_rs.at[i],
                xpeer(i),
            )
        )
    own_copy = pltpu.make_async_copy(
        obs.at[pl.ds(k * share, share)],
        obsx.at[:, pl.ds(pl.multiple_of(k * quarter, quarter), quarter), :],
        own_s,
    )
    own_copy.start()

    loads[7].wait()
    loads[8].wait()
    rows = pl.ds(pl.multiple_of(k * share, share), share)
    labf[...] = lab[rows, :].astype(F32)
    live_col = jnp.transpose(jnp.broadcast_to(live[...], (tiles, tiles)).astype(F32))
    mask[...] = jnp.where(t_row.astype(F32) < live_col, 1.0, 0.0)
    ltile[...] = jnp.zeros_like(ltile)
    for a in range(2):
        rq[a, pl.ds(s_me[a], 1)] = rqs[a, pl.ds(s_me[a], 1)]
        for copy in rq_c[a]:
            copy.wait_recv()
    for a in range(2):
        ask = jnp.sum(rq[a].reshape(NY * NC, slots), axis=0, keepdims=True)
        for b in range(slots // LANES):
            part = jnp.broadcast_to(ask[:, b * LANES : (b + 1) * LANES], (LANES, LANES))
            chosen = jnp.where(part == (t_col + 1).astype(F32), 1.0, 0.0)
            smat_t[a, :, b * LANES : (b + 1) * LANES] = chosen.astype(BF)
            smat[a, b * LANES : (b + 1) * LANES, :] = jnp.transpose(chosen).astype(BF)
    for a in range(2):
        for copy in gat_c[a]:
            copy.wait_recv()
    for a in range(2):
        table = gat[a].reshape(NY * GRP, half_w)
        sels[a] = dot(smat[a], table).astype(BF).reshape(NY * NC, NY * 2, half_w)
    sel_c = []
    for i in s_order:
        for a in range(2):
            q = (s_me[a] + i) % (NY * NC)
            sel_c.append(send(sels.at[a, q], selr.at[a, s_me[a]], sel_ss.at[a, i], sel_rs.at[a, i], s_peer(a, i)))
    for a in range(2):
        selr[a, pl.ds(s_me[a], 1)] = sels[a, pl.ds(s_me[a], 1)]

    for copy in sel_c:
        copy.wait_recv()
    for a in range(2):
        rows_a = dot(tmat[a], selr[a].reshape(slots, half_w)).astype(BF)
        xs[a] = rows_a.reshape(nf, HALVES, part_t, half_w)
    x_c = []
    for h in range(HALVES):
        for i in x_order:
            for a in range(2):
                to = (k + i) % nf
                x_c.append(
                    (h, send(xs.at[a, to, h], xr.at[a, h, k], x_ss.at[a, h, i], x_rs.at[a, h, i], xpeer(i)))
                )
        for a in range(2):
            xr[a, h, pl.ds(k, 1)] = xs[a, pl.ds(k, 1), h]

    lane = lax.broadcasted_iota(jnp.int32, (part_t, LANES), 1) // quarter
    per = LANES // quarter
    lane16 = lax.broadcasted_iota(jnp.int32, (CHAINS, LANES), 1)
    loglik = jnp.zeros((CHAINS, LANES), F32)
    gx_c = []
    for h in range(HALVES):
        for hh, copy in x_c:
            if hh == h:
                copy.wait_recv()
        for a in range(2):
            for b in range(half_w // LANES):
                came = [xr[a, h, kk, :, b * LANES : (b + 1) * LANES].astype(F32) for kk in range(nf)]
                for ci in range(per):
                    out = jnp.zeros((part_t, LANES), F32)
                    for kk in range(nf):
                        shift = ((kk - ci) * quarter) % LANES
                        moved_k = came[kk] if shift == 0 else pltpu.roll(came[kk], shift, 1)
                        out = jnp.where(lane == kk, moved_k, out)
                    chain = a * (CHAINS // 2) + b * per + ci
                    wf[h, chain * part_t : (chain + 1) * part_t, :] = out
        if h == 0:
            own_copy.wait()
            for copy in obs_c:
                copy.wait_recv()
        for n in range(part_t):
            coeff = wf[h, pl.ds(n, CHAINS, stride=part_t), :].astype(BF)
            lg[h, n * CHAINS : (n + 1) * CHAINS, :] = dot(coeff, obsx[h * part_t + n])
        for n in range(part_t):
            t = h * part_t + n
            logits = lg[h, n * CHAINS : (n + 1) * CHAINS, :]
            target = jnp.broadcast_to(labf[t : t + 1, :], (CHAINS, LANES))
            alive = jnp.broadcast_to(mask[pl.ds(k * share + t, 1), :], (CHAINS, LANES)) > 0.5
            e = jnp.exp(-jnp.abs(logits))
            r = 1.0 / (1.0 + e)
            sig = jnp.where(logits >= 0.0, r, e * r)
            res[h, n * CHAINS : (n + 1) * CHAINS, :] = jnp.where(alive, sig - target, 0.0).astype(BF)
            soft = jnp.maximum(logits, 0.0) + jnp.log1p(e)
            term = jnp.where(alive, soft - target * logits, 0.0)
            loglik = jnp.where(lane16 == t, jnp.sum(term, axis=1, keepdims=True), loglik)
        for n in range(part_t):
            back = dot(res[h, n * CHAINS : (n + 1) * CHAINS, :], obsx[h * part_t + n], ((1,), (1,)))
            gf[h, pl.ds(n, CHAINS, stride=part_t), :] = back
        for a in range(2):
            for b in range(half_w // LANES):
                chain = a * (CHAINS // 2) + b * per
                made = [gf[h, (chain + ci) * part_t : (chain + ci + 1) * part_t, :] for ci in range(per)]
                for kk in range(nf):
                    out = jnp.zeros((part_t, LANES), F32)
                    for ci in range(per):
                        shift = ((ci - kk) * quarter) % LANES
                        moved_c = made[ci] if shift == 0 else pltpu.roll(made[ci], shift, 1)
                        out = jnp.where(lane == ci, moved_c, out)
                    gs[a, h, kk, :, b * LANES : (b + 1) * LANES] = out.astype(BF)
        for i in x_order:
            for a in range(2):
                to = (k + i) % nf
                gx_c.append(send(gs.at[a, h, to], gr.at[a, k, h], gx_ss.at[a, h, i], gx_rs.at[a, h, i], xpeer(i)))
        for a in range(2):
            gr[a, pl.ds(k, 1), h] = gs[a, h, pl.ds(k, 1)]

    high = loglik.astype(BF).astype(F32)
    both = jnp.concatenate([high, loglik - high, jnp.zeros((LANES - 2 * CHAINS, LANES), F32)], axis=0)
    ltile[rows, :] = jnp.transpose(both)[:share, :].astype(BF)
    ls[...] = dot(tmat_t[0], ltile[...]).astype(BF).reshape(NY * NC, NY * 2, LANES)
    l_c = []
    for i in s_order:
        q = (s_me[0] + i) % (NY * NC)
        l_c.append(send(ls.at[q], lr.at[s_me[0]], l_ss.at[i], l_rs.at[i], s_peer(0, i)))
    lr[pl.ds(s_me[0], 1)] = ls[pl.ds(s_me[0], 1)]

    for copy in gx_c:
        copy.wait_recv()
    for a in range(2):
        sent = dot(tmat_t[a], gr[a].reshape(tiles, half_w)).astype(BF)
        ms[a] = sent.reshape(NY * NC, NY * 2, half_w)
    m_c = []
    for i in s_order:
        for a in range(2):
            q = (s_me[a] + i) % (NY * NC)
            m_c.append(send(ms.at[a, q], mr.at[a, s_me[a]], m_ss.at[a, i], m_rs.at[a, i], s_peer(a, i)))
    for a in range(2):
        mr[a, pl.ds(s_me[a], 1)] = ms[a, pl.ds(s_me[a], 1)]

    for copy in l_c:
        copy.wait_recv()
    zs[...] = dot(smat_t[0], lr[...].reshape(slots, LANES)).astype(BF).reshape(NY, GRP, LANES)
    z_c = []
    for i in g_order:
        to = (g_me[0] + i) % NY
        z_c.append(send(zs.at[to], zr.at[g_me[0]], z_ss.at[i], z_rs.at[i], g_peer(0, i)))
    zr[pl.ds(g_me[0], 1)] = zs[pl.ds(g_me[0], 1)]

    offset = new_pos[...] - pm[...]
    prior_term = pp * offset
    prior_quad = prior_term * offset

    for copy in m_c:
        copy.wait_recv()
    for a in range(2):
        summed = dot(smat_t[a], mr[a].reshape(slots, half_w)).astype(BF)
        ys[a] = summed.reshape(NY, GRP, half_w)
    y_c = []
    for i in g_order:
        for a in range(2):
            to = (g_me[a] + i) % NY
            y_c.append(send(ys.at[a, to], yr.at[a, g_me[a]], y_ss.at[a, i], y_rs.at[a, i], g_peer(a, i)))
    for a in range(2):
        yr[a, pl.ds(g_me[a], 1)] = ys[a, pl.ds(g_me[a], 1)]

    lik = jnp.zeros((GRP, width), F32)
    group_loglik = jnp.zeros((GRP, LANES), F32)
    for copy in z_c:
        copy.wait_recv()
    for g in range(NY):
        group_loglik = group_loglik + zr[g].astype(F32)
    group_loglik = group_loglik + pltpu.roll(group_loglik, LANES - CHAINS, 1)
    for copy in y_c:
        copy.wait_recv()
    for a in range(2):
        part = yr[a].reshape(NY * GRP, half_w)
        back = dot(part, perm[:, a * half_w : (a + 1) * half_w], ((1,), (1,)))
        for g in range(NY):
            lik = lik + back[g * GRP : (g + 1) * GRP, :]

    grad_now = lik + prior_term
    mom_now = half_s[...] - 0.5 * step_size * grad_now
    new_grd[...] = grad_now
    new_mom[...] = mom_now
    quad = 0.5 * (prior_quad + im * mom_now * mom_now)
    total = quad[:, :LANES]
    for b in range(1, width // LANES):
        total = total + quad[:, b * LANES : (b + 1) * LANES]
    shift = LANES // 2
    while shift >= CHAINS:
        total = total + pltpu.roll(total, shift, 1)
        shift //= 2
    total = total + group_loglik
    er[pl.ds(k, 1)] = total[None]
    e_c = []
    for i in x_order:
        e_c.append(send(er.at[k], er.at[k], e_ss.at[i], e_rs.at[i], xpeer(i)))
    for copy in copies[: -len(e_c)]:
        copy.wait_send()
    for copy in e_c:
        copy.wait_recv()
    whole = er[0]
    for kk in range(1, nf):
        whole = whole + er[kk]
    energy[...] = whole[:, :CHAINS]
    for copy in e_c:
        copy.wait_send()


def hand_over(a, b, c, d, a_out, b_out, c_out, d_out):
    a_out[...] = a[...]
    b_out[...] = b[...]
    c_out[...] = c[...]
    d_out[...] = d[...]


def body(observations, labels, tile_live, tile_group, position, momentum, gradient, prior_mean, prior_prec, inv_mass):
    tiles, quarter, row_count = observations.shape
    groups, width = position.shape
    chains = width // quarter
    nf = lax.axis_size("feat")
    half_w = width // 2
    share = tiles // nf
    S = NY * NC
    part_t = share // HALVES
    V = pltpu.VMEM
    D = pltpu.SemaphoreType.DMA
    S = NY * NC
    scratch = [
        V((tiles, row_count), jnp.int32),
        V((1, tiles), jnp.int32),
        V((1, tiles), jnp.int32),
        V((groups, width), F32),
        V((groups, width), F32),
        V((groups, width), F32),
        V((1, width), F32),
        V((1, quarter), F32),
        V((1, quarter), F32),
        D((10,)),
        V((tiles, quarter, row_count), BF),
        V((share, nf * quarter, row_count), BF),
        V((width, width), BF),
        V((share, row_count), F32),
        V((tiles, LANES), F32),
        V((groups, width), F32),
        V((tiles, LANES), BF),
        V((2, NY, GRP, half_w), BF),
        V((2, S, 1, S * 2 * NY), F32),
        V((2, S, 1, S * 2 * NY), F32),
        V((S * 2 * NY, S * 2 * NY), BF),
        V((2, tiles, S * 2 * NY), BF),
        V((2, S * 2 * NY, tiles), BF),
        V((2, S * 2 * NY, LANES), BF),
        V((2, LANES, S * 2 * NY), BF),
        V((2, S, 2 * NY, half_w), BF),
        V((2, S, 2 * NY, half_w), BF),
        V((2, nf, HALVES, part_t, half_w), BF),
        V((2, HALVES, nf, part_t, half_w), BF),
        V((2, HALVES, nf, part_t, half_w), BF),
        V((2, nf, HALVES, part_t, half_w), BF),
        V((HALVES, CHAINS * part_t, LANES), F32),
        V((HALVES, CHAINS * part_t, LANES), F32),
        V((HALVES, CHAINS * part_t, LANES), F32),
        V((HALVES, CHAINS * part_t, LANES), BF),
        V((2, S, 2 * NY, half_w), BF),
        V((2, S, 2 * NY, half_w), BF),
        V((S, 2 * NY, LANES), BF),
        V((S, 2 * NY, LANES), BF),
        V((NY, GRP, LANES), BF),
        V((NY, GRP, LANES), BF),
        V((2, NY, GRP, half_w), BF),
        V((2, NY, GRP, half_w), BF),
        V((nf, groups, LANES), F32),
        D((nf,)),
        D((nf,)),
        D(()),
        D((2, NY)),
        D((2, NY)),
        D((2, S)),
        D((2, S)),
        D((2, S)),
        D((2, S)),
        D((2, HALVES, nf)),
        D((2, HALVES, nf)),
        D((2, HALVES, nf)),
        D((2, HALVES, nf)),
        D((2, S)),
        D((2, S)),
        D((S,)),
        D((S,)),
        D((NY,)),
        D((NY,)),
        D((2, NY)),
        D((2, NY)),
        D((nf,)),
        D((nf,)),
    ]
    vm = pl.BlockSpec(memory_space=pltpu.VMEM)
    shapes = (
        jax.ShapeDtypeStruct((groups, width), F32),
        jax.ShapeDtypeStruct((groups, width), F32),
        jax.ShapeDtypeStruct((groups, width), F32),
        jax.ShapeDtypeStruct((groups, chains), F32),
    )
    results = pl.pallas_call(
        kernel,
        out_shape=tuple(pltpu.VMEM(x.shape, x.dtype) for x in shapes),
        in_specs=[pl.BlockSpec(memory_space=pltpu.HBM)] * 10,
        out_specs=(vm, vm, vm, vm),
        scratch_shapes=scratch,
        compiler_params=pltpu.CompilerParams(collective_id=0, has_side_effects=True),
        name="leapfrog",
    )(
        observations,
        labels,
        tile_live[None, :],
        tile_group[None, :],
        position,
        momentum,
        gradient,
        prior_mean[None, :],
        prior_prec[None, :],
        inv_mass[None, :],
    )
    return pl.pallas_call(
        hand_over,
        out_shape=shapes,
        in_specs=[vm] * 4,
        out_specs=(vm, vm, vm, vm),
        name="hand_over",
    )(*(pltpu.with_memory_space_constraint(x, pltpu.VMEM) for x in results))


def solution(mesh):
    placed = (
        P("dp", "feat", None),
        P("dp", None),
        P("dp"),
        P("dp"),
        P("dp", "feat"),
        P("dp", "feat"),
        P("dp", "feat"),
        P("feat"),
        P("feat"),
        P("feat"),
    )
    return jax.shard_map(
        body,
        mesh=mesh,
        in_specs=placed,
        out_specs=(P("dp", "feat"), P("dp", "feat"), P("dp", "feat"), P("dp", None)),
        check_vma=False,
    )
```

time: 55.2 us -> 53.4 us (0.967)
  Pallas kernels: 54.1 us -> 52.7 us
    pallas_call x1, Pallas kernels: 1.44 us -> 0.65 us  [body(): pl.pallas_call(hand_over, out_shape=shapes, in_specs=[vm] * 4, out_specs=...]
    pallas_call x1, Pallas kernels: 52.7 us -> 52 us  [body(): pl.pallas_call(kernel, out_shape=tuple((pltpu.VMEM(x.shape, x.dtype) for...]
where the time goes in v3:
time: 53.4 us; the launch traced here: 53.3 us
  Pallas kernels  52.7 us (99%)
  between operations  0.64 us (1%)
    pallas_call x1, Pallas kernels, body(): pl.pallas_call(kernel, out_shape=tuple((pltpu.VMEM(x.shape, x.dtype) for...  52 us

profile of v3, /device:TPU:1, one launch (start us, length us, event | category | flops | bytes accessed | tf_op | source)
XLA Modules:
  0.0 53.3 jit_solution(3268026042151261737)
XLA Ops:
  0.6 52.0 %leapfrog.1 = (f32[16,512]{1,0:T(8,128)S(1)}, f32[16,512]{1,0:T(8,128)S(1)}, f32[16,512]{1,0:T(8,128)S(1)}, f32[16,16]{1,0:T(8,128)S(1)}) custom-call(bf16[128,32,128]{2,1,0:T(8,128)(2,1)} %obs.1, s32[128,128]{1,0:T(8,128)} %lab_h.1, s32[1,128]{1,0:T(1,128)} %bitcast.6, s32[1,128]{1,0:T(1,128)} %bitcast.7, f32[16,512]{1,0:T(8,128)} %pos_h.1, ...), custom_call_target="tpu_custom_call" | custom-call | tf_op jit(solution)/shard_map/leapfrog/pallas_call | solution.py:590
  52.6 0.6 %hand_over.1 = (f32[16,512]{1,0:T(8,128)}, f32[16,512]{1,0:T(8,128)}, f32[16,512]{1,0:T(8,128)}, f32[16,16]{1,0:T(8,128)}) custom-call(f32[16,512]{1,0:T(8,128)S(1)} %get-tuple-element.8.a, f32[16,512]{1,0:T(8,128)S(1)} %get-tuple-element.9.b, f32[16,512]{1,0:T(8,128)S(1)} %get-tuple-element.10.c, f32[16,16]{1,0:T(8,128)S(1)} %get-tuple-element.11.d), custom_call_target="tpu_custom_call" | custom-call | tf_op jit(solution)/shard_map/hand_over/pallas_call | solution.py:610

commit v4 on v3

--- a/solution.py
+++ b/solution.py
@@ -13,7 +13,7 @@
 NY = 8
 NC = 2
 CHAINS = 16
-HALVES = 1
+HALVES = 2
 GRP = 16
 LANES = 128
 BF = jnp.bfloat16
@@ -64,6 +64,10 @@
     mask,
     half_s,
     ltile,
+    lab_r,
+    live_r,
+    lt_s,
+    lt_r,
     gat,
     rqs,
     rq,
@@ -93,7 +97,8 @@
     er,
     obs_ss,
     obs_rs,
-    own_s,
+    lab_ss,
+    lab_rs,
     gat_ss,
     gat_rs,
     rq_ss,
@@ -132,6 +137,9 @@
     def xpeer(i):
         return (d, (k + i) % nf)
 
+    def xcross(i):
+        return (d + 1 - 2 * c, (k + i) % nf)
+
     g_me = (y, z)
     s_me = (z * NC + c, y * NC + c)
 
@@ -144,15 +152,15 @@
 
     x_order = (2, 1, 3)
     g_order = far_first(NY)
+    x_all = x_order + (0,)
     s_order = far_first(NY * NC)
 
     barrier = pltpu.get_barrier_semaphore()
     greet = []
     for i in g_order:
-        greet += [g_peer(0, i), g_peer(1, i)]
-    for i in g_order:
-        greet += [at((y + i) % NY, z, 1 - c), at(y, (z + i) % NY, 1 - c)]
-    greet += [xpeer(i) for i in x_order] + [at(y, z, 1 - c)]
+        for cc in (c, 1 - c):
+            greet += [at((y + i) % NY, z, cc), at(y, (z + i) % NY, cc)]
+    greet += [xpeer(i) for i in x_order] + [xcross(i) for i in x_all]
     for who in greet:
         pl.semaphore_signal(barrier, inc=1, device_id=who, device_id_type=MESH)
     count = len(greet)
@@ -244,18 +252,24 @@
 
     pl.semaphore_wait(barrier, count)
 
-    copies = []
-
     def send(src_ref, dst_ref, ss, rs, who):
         copy = pltpu.make_async_remote_copy(
             src_ref=src_ref, dst_ref=dst_ref, send_sem=ss, recv_sem=rs, device_id=who, device_id_type=MESH
         )
         copy.start()
-        copies.append(copy)
-        return copy
-
-    gat_c = [[], []]
-    rq_c = [[], []]
+
+    def arrived(view, sem):
+        pltpu.make_async_copy(view, view, sem).wait()
+
+    for copy in loads[7:]:
+        copy.wait()
+    mine = pl.ds(pl.multiple_of(k * quarter, quarter), quarter)
+    rows = pl.ds(pl.multiple_of(k * share, share), share)
+    for i in x_all:
+        to = (k + i) % nf
+        send(obs_v.at[pl.ds(to * share, share)], obsx.at[:, mine, :], obs_ss, obs_rs, xcross(i))
+    send(lab.at[rows], lab_r, lab_ss.at[0], lab_rs.at[0], xcross(0))
+    send(live, live_r, lab_ss.at[1], lab_rs.at[1], xcross(0))
     hops = {}
     for i in s_order:
         hops.setdefault(min(i // NC, NY - i // NC), []).append(i)
@@ -263,45 +277,15 @@
         for i in hops[far]:
             for a in range(2):
                 q = (s_me[a] + i) % (NY * NC)
-                rq_c[a].append(
-                    send(rqs.at[a, q], rq.at[a, s_me[a]], rq_ss.at[a, i], rq_rs.at[a, i], s_peer(a, i))
-                )
+                send(rqs.at[a, q], rq.at[a, s_me[a]], rq_ss, rq_rs, s_peer(a, i))
         for i in g_order:
             if min(i, NY - i) == far:
                 for a in range(2):
                     ref = gat.at[a, g_me[a]]
-                    gat_c[a].append(send(ref, ref, gat_ss.at[a, i], gat_rs.at[a, i], g_peer(a, i)))
-    loads[9].wait()
-    obs_c = []
-    for i in x_order:
-        to = (k + i) % nf
-        obs_c.append(
-            send(
-                obs_v.at[pl.ds(to * share, share)],
-                obsx.at[:, pl.ds(pl.multiple_of(k * quarter, quarter), quarter), :],
-                obs_ss.at[i],
-                obs_rs.at[i],
-                xpeer(i),
-            )
-        )
-    own_copy = pltpu.make_async_copy(
-        obs.at[pl.ds(k * share, share)],
-        obsx.at[:, pl.ds(pl.multiple_of(k * quarter, quarter), quarter), :],
-        own_s,
-    )
-    own_copy.start()
-
-    loads[7].wait()
-    loads[8].wait()
-    rows = pl.ds(pl.multiple_of(k * share, share), share)
-    labf[...] = lab[rows, :].astype(F32)
-    live_col = jnp.transpose(jnp.broadcast_to(live[...], (tiles, tiles)).astype(F32))
-    mask[...] = jnp.where(t_row.astype(F32) < live_col, 1.0, 0.0)
-    ltile[...] = jnp.zeros_like(ltile)
+                    send(ref, ref, gat_ss, gat_rs, g_peer(a, i))
     for a in range(2):
         rq[a, pl.ds(s_me[a], 1)] = rqs[a, pl.ds(s_me[a], 1)]
-        for copy in rq_c[a]:
-            copy.wait_recv()
+    arrived(rq.at[:, pl.ds(0, NY * NC - 1)], rq_rs)
     for a in range(2):
         ask = jnp.sum(rq[a].reshape(NY * NC, slots), axis=0, keepdims=True)
         for b in range(slots // LANES):
@@ -309,45 +293,40 @@
             chosen = jnp.where(part == (t_col + 1).astype(F32), 1.0, 0.0)
             smat_t[a, :, b * LANES : (b + 1) * LANES] = chosen.astype(BF)
             smat[a, b * LANES : (b + 1) * LANES, :] = jnp.transpose(chosen).astype(BF)
-    for a in range(2):
-        for copy in gat_c[a]:
-            copy.wait_recv()
+    arrived(gat.at[:, pl.ds(0, NY - 1)], gat_rs)
     for a in range(2):
         table = gat[a].reshape(NY * GRP, half_w)
         sels[a] = dot(smat[a], table).astype(BF).reshape(NY * NC, NY * 2, half_w)
-    sel_c = []
     for i in s_order:
         for a in range(2):
             q = (s_me[a] + i) % (NY * NC)
-            sel_c.append(send(sels.at[a, q], selr.at[a, s_me[a]], sel_ss.at[a, i], sel_rs.at[a, i], s_peer(a, i)))
+            send(sels.at[a, q], selr.at[a, s_me[a]], sel_ss, sel_rs, s_peer(a, i))
     for a in range(2):
         selr[a, pl.ds(s_me[a], 1)] = sels[a, pl.ds(s_me[a], 1)]
 
-    for copy in sel_c:
-        copy.wait_recv()
+    arrived(lab_r, lab_rs.at[0])
+    arrived(live_r, lab_rs.at[1])
+    labf[...] = lab_r[...].astype(F32)
+    live_col = jnp.transpose(jnp.broadcast_to(live_r[...], (tiles, tiles)).astype(F32))
+    mask[...] = jnp.where(t_row.astype(F32) < live_col, 1.0, 0.0)
+    ltile[...] = jnp.zeros_like(ltile)
+
+    arrived(selr.at[:, pl.ds(0, NY * NC - 1)], sel_rs)
     for a in range(2):
         rows_a = dot(tmat[a], selr[a].reshape(slots, half_w)).astype(BF)
         xs[a] = rows_a.reshape(nf, HALVES, part_t, half_w)
-    x_c = []
     for h in range(HALVES):
-        for i in x_order:
+        for i in x_all:
             for a in range(2):
                 to = (k + i) % nf
-                x_c.append(
-                    (h, send(xs.at[a, to, h], xr.at[a, h, k], x_ss.at[a, h, i], x_rs.at[a, h, i], xpeer(i)))
-                )
-        for a in range(2):
-            xr[a, h, pl.ds(k, 1)] = xs[a, pl.ds(k, 1), h]
+                send(xs.at[a, to, h], xr.at[a, h, k], x_ss, x_rs.at[h], xcross(i))
 
     lane = lax.broadcasted_iota(jnp.int32, (part_t, LANES), 1) // quarter
     per = LANES // quarter
     lane16 = lax.broadcasted_iota(jnp.int32, (CHAINS, LANES), 1)
     loglik = jnp.zeros((CHAINS, LANES), F32)
-    gx_c = []
     for h in range(HALVES):
-        for hh, copy in x_c:
-            if hh == h:
-                copy.wait_recv()
+        arrived(xr.at[:, h], x_rs.at[h])
         for a in range(2):
             for b in range(half_w // LANES):
                 came = [xr[a, h, kk, :, b * LANES : (b + 1) * LANES].astype(F32) for kk in range(nf)]
@@ -360,9 +339,7 @@
                     chain = a * (CHAINS // 2) + b * per + ci
                     wf[h, chain * part_t : (chain + 1) * part_t, :] = out
         if h == 0:
-            own_copy.wait()
-            for copy in obs_c:
-                copy.wait_recv()
+            arrived(obsx, obs_rs)
         for n in range(part_t):
             coeff = wf[h, pl.ds(n, CHAINS, stride=part_t), :].astype(BF)
             lg[h, n * CHAINS : (n + 1) * CHAINS, :] = dot(coeff, obsx[h * part_t + n])
@@ -392,71 +369,63 @@
                         moved_c = made[ci] if shift == 0 else pltpu.roll(made[ci], shift, 1)
                         out = jnp.where(lane == ci, moved_c, out)
                     gs[a, h, kk, :, b * LANES : (b + 1) * LANES] = out.astype(BF)
-        for i in x_order:
+        for i in x_all:
             for a in range(2):
                 to = (k + i) % nf
-                gx_c.append(send(gs.at[a, h, to], gr.at[a, k, h], gx_ss.at[a, h, i], gx_rs.at[a, h, i], xpeer(i)))
-        for a in range(2):
-            gr[a, pl.ds(k, 1), h] = gs[a, h, pl.ds(k, 1)]
+                send(gs.at[a, h, to], gr.at[a, k, h], gx_ss, gx_rs, xcross(i))
 
     high = loglik.astype(BF).astype(F32)
     both = jnp.concatenate([high, loglik - high, jnp.zeros((LANES - 2 * CHAINS, LANES), F32)], axis=0)
-    ltile[rows, :] = jnp.transpose(both)[:share, :].astype(BF)
+    lt_s[...] = jnp.transpose(both)[:share, :].astype(BF)
+    send(lt_s, lt_r, lab_ss.at[2], lab_rs.at[2], xcross(0))
+    arrived(lt_r, lab_rs.at[2])
+    ltile[rows, :] = lt_r[...]
     ls[...] = dot(tmat_t[0], ltile[...]).astype(BF).reshape(NY * NC, NY * 2, LANES)
-    l_c = []
     for i in s_order:
         q = (s_me[0] + i) % (NY * NC)
-        l_c.append(send(ls.at[q], lr.at[s_me[0]], l_ss.at[i], l_rs.at[i], s_peer(0, i)))
+        send(ls.at[q], lr.at[s_me[0]], l_ss, l_rs, s_peer(0, i))
     lr[pl.ds(s_me[0], 1)] = ls[pl.ds(s_me[0], 1)]
 
-    for copy in gx_c:
-        copy.wait_recv()
+    arrived(gr, gx_rs)
     for a in range(2):
         sent = dot(tmat_t[a], gr[a].reshape(tiles, half_w)).astype(BF)
         ms[a] = sent.reshape(NY * NC, NY * 2, half_w)
-    m_c = []
     for i in s_order:
         for a in range(2):
             q = (s_me[a] + i) % (NY * NC)
-            m_c.append(send(ms.at[a, q], mr.at[a, s_me[a]], m_ss.at[a, i], m_rs.at[a, i], s_peer(a, i)))
+            send(ms.at[a, q], mr.at[a, s_me[a]], m_ss, m_rs, s_peer(a, i))
     for a in range(2):
         mr[a, pl.ds(s_me[a], 1)] = ms[a, pl.ds(s_me[a], 1)]
 
-    for copy in l_c:
-        copy.wait_recv()
+    arrived(lr.at[pl.ds(0, NY * NC - 1)], l_rs)
     zs[...] = dot(smat_t[0], lr[...].reshape(slots, LANES)).astype(BF).reshape(NY, GRP, LANES)
-    z_c = []
     for i in g_order:
         to = (g_me[0] + i) % NY
-        z_c.append(send(zs.at[to], zr.at[g_me[0]], z_ss.at[i], z_rs.at[i], g_peer(0, i)))
+        send(zs.at[to], zr.at[g_me[0]], z_ss, z_rs, g_peer(0, i))
     zr[pl.ds(g_me[0], 1)] = zs[pl.ds(g_me[0], 1)]
 
     offset = new_pos[...] - pm[...]
     prior_term = pp * offset
     prior_quad = prior_term * offset
 
-    for copy in m_c:
-        copy.wait_recv()
+    arrived(mr.at[:, pl.ds(0, NY * NC - 1)], m_rs)
     for a in range(2):
         summed = dot(smat_t[a], mr[a].reshape(slots, half_w)).astype(BF)
         ys[a] = summed.reshape(NY, GRP, half_w)
-    y_c = []
     for i in g_order:
         for a in range(2):
             to = (g_me[a] + i) % NY
-            y_c.append(send(ys.at[a, to], yr.at[a, g_me[a]], y_ss.at[a, i], y_rs.at[a, i], g_peer(a, i)))
+            send(ys.at[a, to], yr.at[a, g_me[a]], y_ss, y_rs, g_peer(a, i))
     for a in range(2):
         yr[a, pl.ds(g_me[a], 1)] = ys[a, pl.ds(g_me[a], 1)]
 
     lik = jnp.zeros((GRP, width), F32)
     group_loglik = jnp.zeros((GRP, LANES), F32)
-    for copy in z_c:
-        copy.wait_recv()
+    arrived(zr.at[pl.ds(0, NY - 1)], z_rs)
     for g in range(NY):
         group_loglik = group_loglik + zr[g].astype(F32)
     group_loglik = group_loglik + pltpu.roll(group_loglik, LANES - CHAINS, 1)
-    for copy in y_c:
-        copy.wait_recv()
+    arrived(yr.at[:, pl.ds(0, NY - 1)], y_rs)
     for a in range(2):
         part = yr[a].reshape(NY * GRP, half_w)
         back = dot(part, perm[:, a * half_w : (a + 1) * half_w], ((1,), (1,)))
@@ -477,19 +446,30 @@
         shift //= 2
     total = total + group_loglik
     er[pl.ds(k, 1)] = total[None]
-    e_c = []
     for i in x_order:
-        e_c.append(send(er.at[k], er.at[k], e_ss.at[i], e_rs.at[i], xpeer(i)))
-    for copy in copies[: -len(e_c)]:
-        copy.wait_send()
-    for copy in e_c:
-        copy.wait_recv()
+        send(er.at[k], er.at[k], e_ss, e_rs, xpeer(i))
+    for view, sem in (
+        (obs_v, obs_ss),
+        (rq.at[:, pl.ds(0, NY * NC - 1)], rq_ss),
+        (gat.at[:, pl.ds(0, NY - 1)], gat_ss),
+        (sels.at[:, pl.ds(0, NY * NC - 1)], sel_ss),
+        (xs, x_ss),
+        (gs, gx_ss),
+        (ls.at[pl.ds(0, NY * NC - 1)], l_ss),
+        (ms.at[:, pl.ds(0, NY * NC - 1)], m_ss),
+        (zs.at[pl.ds(0, NY - 1)], z_ss),
+        (ys.at[:, pl.ds(0, NY - 1)], y_ss),
+        (lab_r, lab_ss.at[0]),
+        (live_r, lab_ss.at[1]),
+        (lt_s, lab_ss.at[2]),
+    ):
+        arrived(view, sem)
+    arrived(er.at[pl.ds(0, nf - 1)], e_rs)
     whole = er[0]
     for kk in range(1, nf):
         whole = whole + er[kk]
     energy[...] = whole[:, :CHAINS]
-    for copy in e_c:
-        copy.wait_send()
+    arrived(er.at[pl.ds(0, nf - 1)], e_ss)
 
 
 def hand_over(a, b, c, d, a_out, b_out, c_out, d_out):
@@ -529,6 +509,10 @@
         V((tiles, LANES), F32),
         V((groups, width), F32),
         V((tiles, LANES), BF),
+        V((share, row_count), jnp.int32),
+        V((1, tiles), jnp.int32),
+        V((share, LANES), BF),
+        V((share, LANES), BF),
         V((2, NY, GRP, half_w), BF),
         V((2, S, 1, S * 2 * NY), F32),
         V((2, S, 1, S * 2 * NY), F32),
@@ -556,29 +540,30 @@
         V((2, NY, GRP, half_w), BF),
         V((2, NY, GRP, half_w), BF),
         V((nf, groups, LANES), F32),
-        D((nf,)),
-        D((nf,)),
-        D(()),
-        D((2, NY)),
-        D((2, NY)),
-        D((2, S)),
-        D((2, S)),
-        D((2, S)),
-        D((2, S)),
-        D((2, HALVES, nf)),
-        D((2, HALVES, nf)),
-        D((2, HALVES, nf)),
-        D((2, HALVES, nf)),
-        D((2, S)),
-        D((2, S)),
-        D((S,)),
-        D((S,)),
-        D((NY,)),
-        D((NY,)),
-        D((2, NY)),
-        D((2, NY)),
-        D((nf,)),
-        D((nf,)),
+        D(()),
+        D(()),
+        D((3,)),
+        D((3,)),
+        D(()),
+        D(()),
+        D(()),
+        D(()),
+        D(()),
+        D(()),
+        D(()),
+        D((HALVES,)),
+        D(()),
+        D(()),
+        D(()),
+        D(()),
+        D(()),
+        D(()),
+        D(()),
+        D(()),
+        D(()),
+        D(()),
+        D(()),
+        D(()),
     ]
     vm = pl.BlockSpec(memory_space=pltpu.VMEM)
     shapes = (

time: 53.4 us -> 49.8 us (0.933)
  Pallas kernels: 52.7 us -> 49.1 us
    pallas_call x1, Pallas kernels: 52 us -> 48.4 us  [body(): pl.pallas_call(kernel, out_shape=tuple((pltpu.VMEM(x.shape, x.dtype) for...]
where the time goes in v4:
time: 49.8 us; the launch traced here: 49.7 us
  Pallas kernels  49.1 us (99%)
  between operations  0.64 us (1%)
    pallas_call x1, Pallas kernels, body(): pl.pallas_call(kernel, out_shape=tuple((pltpu.VMEM(x.shape, x.dtype) for...  48.4 us

profile of v4, /device:TPU:1, one launch (start us, length us, event | category | flops | bytes accessed | tf_op | source)
XLA Modules:
  0.0 49.7 jit_solution(11157167256889105314)
XLA Ops:
  0.6 48.4 %leapfrog.1 = (f32[16,512]{1,0:T(8,128)S(1)}, f32[16,512]{1,0:T(8,128)S(1)}, f32[16,512]{1,0:T(8,128)S(1)}, f32[16,16]{1,0:T(8,128)S(1)}) custom-call(bf16[128,32,128]{2,1,0:T(8,128)(2,1)} %obs.1, s32[128,128]{1,0:T(8,128)} %lab_h.1, s32[1,128]{1,0:T(1,128)} %bitcast.6, s32[1,128]{1,0:T(1,128)} %bitcast.7, f32[16,512]{1,0:T(8,128)} %pos_h.1, ...), custom_call_target="tpu_custom_call" | custom-call | tf_op jit(solution)/shard_map/leapfrog/pallas_call | solution.py:575
  49.1 0.6 %hand_over.1 = (f32[16,512]{1,0:T(8,128)}, f32[16,512]{1,0:T(8,128)}, f32[16,512]{1,0:T(8,128)}, f32[16,16]{1,0:T(8,128)}) custom-call(f32[16,512]{1,0:T(8,128)S(1)} %get-tuple-element.8.a, f32[16,512]{1,0:T(8,128)S(1)} %get-tuple-element.9.b, f32[16,512]{1,0:T(8,128)S(1)} %get-tuple-element.10.c, f32[16,16]{1,0:T(8,128)S(1)} %get-tuple-element.11.d), custom_call_target="tpu_custom_call" | custom-call | tf_op jit(solution)/shard_map/hand_over/pallas_call | solution.py:595

commit v5 on v4

--- a/solution.py
+++ b/solution.py
@@ -224,12 +224,13 @@
     rank_row = jnp.broadcast_to(rank_row, (tiles, tiles))
     rank_col = jnp.transpose(rank_row).astype(jnp.int32)
     rank_row = rank_row.astype(jnp.int32)
-    slots = NY * NC * NY * 2
+    nq = NY * NC
+    slots = nq * NY * 2
 
     def slot_of(a, own, rank):
         oy, oz, oc = own // (NY * NC), (own // NC) % NY, own % NC
         first, second = (oy, oz) if a == 0 else (oz, oy)
-        return (second * NC + oc) * (NY * 2) + first * 2 + rank, first
+        return (second * NC + oc + nq - s_me[a]) % nq * (NY * 2) + first * 2 + rank, first
 
     for b in range(slots // LANES):
         here = lax.broadcasted_iota(jnp.int32, (LANES, slots), 0) + b * LANES
@@ -246,7 +247,7 @@
             tmat_t[a, b * LANES : (b + 1) * LANES, :] = one_hot(s_r == t_col + b * LANES)
         wanted = jnp.broadcast_to(dot(asked, tmat[a])[:1, :], (NY * NC, slots))
         spread_q = dot(jnp.where(lane_q == row_q, wanted, 0.0).astype(BF), fold[...])
-        placed = jnp.where(lane_q == s_me[a], spread_q, 0.0)
+        placed = jnp.where(lane_q == (nq - row_q) % nq, spread_q, 0.0)
         for q in range(NY * NC):
             rqs[a, q] = placed[q : q + 1, :]
 
@@ -276,15 +277,14 @@
     for far in sorted(hops, reverse=True):
         for i in hops[far]:
             for a in range(2):
-                q = (s_me[a] + i) % (NY * NC)
-                send(rqs.at[a, q], rq.at[a, s_me[a]], rq_ss, rq_rs, s_peer(a, i))
+                send(rqs.at[a, i], rq.at[a, nq - i], rq_ss, rq_rs, s_peer(a, i))
         for i in g_order:
             if min(i, NY - i) == far:
                 for a in range(2):
                     ref = gat.at[a, g_me[a]]
                     send(ref, ref, gat_ss, gat_rs, g_peer(a, i))
     for a in range(2):
-        rq[a, pl.ds(s_me[a], 1)] = rqs[a, pl.ds(s_me[a], 1)]
+        rq[a, 0] = rqs[a, 0]
     arrived(rq.at[:, pl.ds(0, NY * NC - 1)], rq_rs)
     for a in range(2):
         ask = jnp.sum(rq[a].reshape(NY * NC, slots), axis=0, keepdims=True)
@@ -294,15 +294,18 @@
             smat_t[a, :, b * LANES : (b + 1) * LANES] = chosen.astype(BF)
             smat[a, b * LANES : (b + 1) * LANES, :] = jnp.transpose(chosen).astype(BF)
     arrived(gat.at[:, pl.ds(0, NY - 1)], gat_rs)
-    for a in range(2):
-        table = gat[a].reshape(NY * GRP, half_w)
-        sels[a] = dot(smat[a], table).astype(BF).reshape(NY * NC, NY * 2, half_w)
-    for i in s_order:
+    far_q, near_q = (i for i in s_order if 4 <= i <= 12), (i for i in s_order if not 4 <= i <= 12)
+    for span, targets in ((((4, 13),), far_q), (((0, 4), (13, nq)), near_q)):
         for a in range(2):
-            q = (s_me[a] + i) % (NY * NC)
-            send(sels.at[a, q], selr.at[a, s_me[a]], sel_ss, sel_rs, s_peer(a, i))
-    for a in range(2):
-        selr[a, pl.ds(s_me[a], 1)] = sels[a, pl.ds(s_me[a], 1)]
+            table = gat[a].reshape(NY * GRP, half_w)
+            for lo, hi in span:
+                picked = dot(smat[a, lo * 2 * NY : hi * 2 * NY, :], table).astype(BF)
+                sels[a, lo:hi] = picked.reshape(hi - lo, NY * 2, half_w)
+        for i in targets:
+            for a in range(2):
+                send(sels.at[a, i], selr.at[a, nq - i], sel_ss, sel_rs, s_peer(a, i))
+    for a in range(2):
+        selr[a, 0] = sels[a, 0]
 
     arrived(lab_r, lab_rs.at[0])
     arrived(live_r, lab_rs.at[1])
@@ -382,20 +385,22 @@
     ltile[rows, :] = lt_r[...]
     ls[...] = dot(tmat_t[0], ltile[...]).astype(BF).reshape(NY * NC, NY * 2, LANES)
     for i in s_order:
-        q = (s_me[0] + i) % (NY * NC)
-        send(ls.at[q], lr.at[s_me[0]], l_ss, l_rs, s_peer(0, i))
-    lr[pl.ds(s_me[0], 1)] = ls[pl.ds(s_me[0], 1)]
+        send(ls.at[i], lr.at[nq - i], l_ss, l_rs, s_peer(0, i))
+    lr[0] = ls[0]
 
     arrived(gr, gx_rs)
-    for a in range(2):
-        sent = dot(tmat_t[a], gr[a].reshape(tiles, half_w)).astype(BF)
-        ms[a] = sent.reshape(NY * NC, NY * 2, half_w)
-    for i in s_order:
+    far_q, near_q = (i for i in s_order if 4 <= i <= 12), (i for i in s_order if not 4 <= i <= 12)
+    for span, targets in ((((4, 13),), far_q), (((0, 4), (13, nq)), near_q)):
         for a in range(2):
-            q = (s_me[a] + i) % (NY * NC)
-            send(ms.at[a, q], mr.at[a, s_me[a]], m_ss, m_rs, s_peer(a, i))
-    for a in range(2):
-        mr[a, pl.ds(s_me[a], 1)] = ms[a, pl.ds(s_me[a], 1)]
+            came = gr[a].reshape(tiles, half_w)
+            for lo, hi in span:
+                sent = dot(tmat_t[a, lo * 2 * NY : hi * 2 * NY, :], came).astype(BF)
+                ms[a, lo:hi] = sent.reshape(hi - lo, NY * 2, half_w)
+        for i in targets:
+            for a in range(2):
+                send(ms.at[a, i], mr.at[a, nq - i], m_ss, m_rs, s_peer(a, i))
+    for a in range(2):
+        mr[a, 0] = ms[a, 0]
 
     arrived(lr.at[pl.ds(0, NY * NC - 1)], l_rs)
     zs[...] = dot(smat_t[0], lr[...].reshape(slots, LANES)).astype(BF).reshape(NY, GRP, LANES)
@@ -434,8 +439,6 @@
 
     grad_now = lik + prior_term
     mom_now = half_s[...] - 0.5 * step_size * grad_now
-    new_grd[...] = grad_now
-    new_mom[...] = mom_now
     quad = 0.5 * (prior_quad + im * mom_now * mom_now)
     total = quad[:, :LANES]
     for b in range(1, width // LANES):
@@ -448,6 +451,8 @@
     er[pl.ds(k, 1)] = total[None]
     for i in x_order:
         send(er.at[k], er.at[k], e_ss, e_rs, xpeer(i))
+    new_grd[...] = grad_now
+    new_mom[...] = mom_now
     for view, sem in (
         (obs_v, obs_ss),
         (rq.at[:, pl.ds(0, NY * NC - 1)], rq_ss),

time: 49.8 us -> 49.5 us (level)
  no operation moved by 1% of the time
where the time goes in v5:
time: 49.5 us; the launch traced here: 49.4 us
  Pallas kernels  48.7 us (98%)
  between operations  0.64 us (1%)
    pallas_call x1, Pallas kernels, body(): pl.pallas_call(kernel, out_shape=tuple((pltpu.VMEM(x.shape, x.dtype) for...  48.1 us

profile of v5, /device:TPU:1, one launch (start us, length us, event | category | flops | bytes accessed | tf_op | source)
XLA Modules:
  0.0 49.4 jit_solution(5252262885871469046)
XLA Ops:
  0.6 48.1 %leapfrog.1 = (f32[16,512]{1,0:T(8,128)S(1)}, f32[16,512]{1,0:T(8,128)S(1)}, f32[16,512]{1,0:T(8,128)S(1)}, f32[16,16]{1,0:T(8,128)S(1)}) custom-call(bf16[128,32,128]{2,1,0:T(8,128)(2,1)} %obs.1, s32[128,128]{1,0:T(8,128)} %lab_h.1, s32[1,128]{1,0:T(1,128)} %bitcast.6, s32[1,128]{1,0:T(1,128)} %bitcast.7, f32[16,512]{1,0:T(8,128)} %pos_h.1, ...), custom_call_target="tpu_custom_call" | custom-call | tf_op jit(solution)/shard_map/leapfrog/pallas_call | solution.py:580
  48.7 0.6 %hand_over.1 = (f32[16,512]{1,0:T(8,128)}, f32[16,512]{1,0:T(8,128)}, f32[16,512]{1,0:T(8,128)}, f32[16,16]{1,0:T(8,128)}) custom-call(f32[16,512]{1,0:T(8,128)S(1)} %get-tuple-element.8.a, f32[16,512]{1,0:T(8,128)S(1)} %get-tuple-element.9.b, f32[16,512]{1,0:T(8,128)S(1)} %get-tuple-element.10.c, f32[16,16]{1,0:T(8,128)S(1)} %get-tuple-element.11.d), custom_call_target="tpu_custom_call" | custom-call | tf_op jit(solution)/shard_map/hand_over/pallas_call | solution.py:600

commit v6 on v5

--- a/solution.py
+++ b/solution.py
@@ -211,7 +211,7 @@
     new_pos[...] = moved
     block = dot(moved.astype(BF), perm[...]).astype(BF)
     for a in range(2):
-        gat[a, pl.ds(g_me[a], 1)] = block[None, :, a * half_w : (a + 1) * half_w]
+        gat[a, 0] = block[:, a * half_w : (a + 1) * half_w]
 
     loads[0].wait()
     tile_row = jnp.broadcast_to(tg[...], (tiles, tiles))
@@ -240,7 +240,7 @@
     row_q = lax.broadcasted_iota(jnp.int32, (NY * NC, slots), 0)
     for a in range(2):
         s_r, first = slot_of(a, own_row, rank_row)
-        asked = (first * GRP + tile_row % GRP + 1)[:16, :].astype(F32).astype(BF)
+        asked = ((first + NY - g_me[a]) % NY * GRP + tile_row % GRP + 1)[:16, :].astype(F32).astype(BF)
         s_c, _ = slot_of(a, own_col, rank_col)
         for b in range(slots // LANES):
             tmat[a, :, b * LANES : (b + 1) * LANES] = one_hot(s_c == t_row + b * LANES)
@@ -281,8 +281,7 @@
         for i in g_order:
             if min(i, NY - i) == far:
                 for a in range(2):
-                    ref = gat.at[a, g_me[a]]
-                    send(ref, ref, gat_ss, gat_rs, g_peer(a, i))
+                    send(gat.at[a, 0], gat.at[a, NY - i], gat_ss, gat_rs, g_peer(a, i))
     for a in range(2):
         rq[a, 0] = rqs[a, 0]
     arrived(rq.at[:, pl.ds(0, NY * NC - 1)], rq_rs)
@@ -405,24 +404,26 @@
     arrived(lr.at[pl.ds(0, NY * NC - 1)], l_rs)
     zs[...] = dot(smat_t[0], lr[...].reshape(slots, LANES)).astype(BF).reshape(NY, GRP, LANES)
     for i in g_order:
-        to = (g_me[0] + i) % NY
-        send(zs.at[to], zr.at[g_me[0]], z_ss, z_rs, g_peer(0, i))
-    zr[pl.ds(g_me[0], 1)] = zs[pl.ds(g_me[0], 1)]
+        send(zs.at[i], zr.at[NY - i], z_ss, z_rs, g_peer(0, i))
+    zr[0] = zs[0]
 
     offset = new_pos[...] - pm[...]
     prior_term = pp * offset
     prior_quad = prior_term * offset
 
     arrived(mr.at[:, pl.ds(0, NY * NC - 1)], m_rs)
-    for a in range(2):
-        summed = dot(smat_t[a], mr[a].reshape(slots, half_w)).astype(BF)
-        ys[a] = summed.reshape(NY, GRP, half_w)
-    for i in g_order:
+    for span, near in ((((2, 7),), False), (((0, 2), (7, NY)), True)):
         for a in range(2):
-            to = (g_me[a] + i) % NY
-            send(ys.at[a, to], yr.at[a, g_me[a]], y_ss, y_rs, g_peer(a, i))
-    for a in range(2):
-        yr[a, pl.ds(g_me[a], 1)] = ys[a, pl.ds(g_me[a], 1)]
+            came = mr[a].reshape(slots, half_w)
+            for lo, hi in span:
+                summed = dot(smat_t[a, lo * GRP : hi * GRP, :], came).astype(BF)
+                ys[a, lo:hi] = summed.reshape(hi - lo, GRP, half_w)
+        for i in g_order:
+            if (min(i, NY - i) == 1) == near:
+                for a in range(2):
+                    send(ys.at[a, i], yr.at[a, NY - i], y_ss, y_rs, g_peer(a, i))
+    for a in range(2):
+        yr[a, 0] = ys[a, 0]
 
     lik = jnp.zeros((GRP, width), F32)
     group_loglik = jnp.zeros((GRP, LANES), F32)

time: 49.5 us -> 49.6 us (level)
  no operation moved by 1% of the time
where the time goes in v6:
time: 49.6 us; the launch traced here: 49.5 us
  Pallas kernels  48.8 us (98%)
  between operations  0.64 us (1%)
    pallas_call x1, Pallas kernels, body(): pl.pallas_call(kernel, out_shape=tuple((pltpu.VMEM(x.shape, x.dtype) for...  48.2 us

profile of v6, /device:TPU:1, one launch (start us, length us, event | category | flops | bytes accessed | tf_op | source)
XLA Modules:
  0.0 49.5 jit_solution(15317506182143781091)
XLA Ops:
  0.6 48.2 %leapfrog.1 = (f32[16,512]{1,0:T(8,128)S(1)}, f32[16,512]{1,0:T(8,128)S(1)}, f32[16,512]{1,0:T(8,128)S(1)}, f32[16,16]{1,0:T(8,128)S(1)}) custom-call(bf16[128,32,128]{2,1,0:T(8,128)(2,1)} %obs.1, s32[128,128]{1,0:T(8,128)} %lab_h.1, s32[1,128]{1,0:T(1,128)} %bitcast.6, s32[1,128]{1,0:T(1,128)} %bitcast.7, f32[16,512]{1,0:T(8,128)} %pos_h.1, ...), custom_call_target="tpu_custom_call" | custom-call | tf_op jit(solution)/shard_map/leapfrog/pallas_call | solution.py:581
  48.8 0.6 %hand_over.1 = (f32[16,512]{1,0:T(8,128)}, f32[16,512]{1,0:T(8,128)}, f32[16,512]{1,0:T(8,128)}, f32[16,16]{1,0:T(8,128)}) custom-call(f32[16,512]{1,0:T(8,128)S(1)} %get-tuple-element.8.a, f32[16,512]{1,0:T(8,128)S(1)} %get-tuple-element.9.b, f32[16,512]{1,0:T(8,128)S(1)} %get-tuple-element.10.c, f32[16,16]{1,0:T(8,128)S(1)} %get-tuple-element.11.d), custom_call_target="tpu_custom_call" | custom-call | tf_op jit(solution)/shard_map/hand_over/pallas_call | solution.py:601
